TPU v7x, 16 devices: a whole 2x2x2 slice. The times are simulated.
16 devices in a mesh: rep: 1, dp: 16 (over x, y, z, core).
Axes of the slice: x: 2, y: 2, z: 2, core: 2. Of those that a mesh axis runs over, the one named last changes fastest.
Arguments:
- x: bfloat16 [16, 2048, 1536], P(('rep', 'dp'))
- dy: bfloat16 [16, 2048, 1536], P(('rep', 'dp'))
- w_gate: bfloat16 [2, 1536, 4096], P(None, 'dp')
- w_up: bfloat16 [2, 1536, 4096], P(None, 'dp')
- w_down: bfloat16 [2, 4096, 1536], P(None, 'dp')
- m_w_gate: float32 [2, 1536, 4096], P(None, 'dp')
- m_w_up: float32 [2, 1536, 4096], P(None, 'dp')
- m_w_down: float32 [2, 4096, 1536], P(None, 'dp')
- v_w_gate: float32 [2, 1536, 4096], P(None, 'dp')
- v_w_up: float32 [2, 1536, 4096], P(None, 'dp')
- v_w_down: float32 [2, 4096, 1536], P(None, 'dp')
Outputs:
- output 1: bfloat16 [2, 1536, 4096], P('rep', 'dp')
- output 2: bfloat16 [2, 1536, 4096], P('rep', 'dp')
- output 3: bfloat16 [2, 4096, 1536], P('rep', 'dp')
- output 4: float32 [2, 1536, 4096], P('rep', 'dp')
- output 5: float32 [2, 1536, 4096], P('rep', 'dp')
- output 6: float32 [2, 4096, 1536], P('rep', 'dp')
- output 7: float32 [2, 1536, 4096], P('rep', 'dp')
- output 8: float32 [2, 1536, 4096], P('rep', 'dp')
- output 9: float32 [2, 4096, 1536], P('rep', 'dp')
All inputs are finite; a program needn't handle non-finite values.
Results may differ from a plain program's by a relative error of at most 0.022.
Values are sent between devices in bfloat16 or wider.
A program may use at most 2 GiB of HBM per device.

v0:
```python
import jax
import jax.numpy as jnp
from jax import lax
from jax.sharding import PartitionSpec as P

NAMES = ("w_gate", "w_up", "w_down")


def matmul(a, w):
    return jnp.dot(a, w, preferred_element_type=jnp.float32).astype(jnp.bfloat16)


def normed(h):
    wide = h.astype(jnp.float32)
    scale = lax.rsqrt(jnp.mean(wide**2, -1, keepdims=True) + 1e-6)
    return (wide * scale).astype(jnp.bfloat16)


def layer(h, w):
    a = normed(h)
    gate = jnp.dot(a, w["w_gate"], preferred_element_type=jnp.float32)
    up = jnp.dot(a, w["w_up"], preferred_element_type=jnp.float32)
    return h + matmul((jax.nn.silu(gate) * up).astype(jnp.bfloat16), w["w_down"])


def adamw(w, m, v, g):
    m = 0.9 * m + 0.1 * g
    v = 0.95 * v + 0.05 * g * g
    step = m * lax.rsqrt(v + 1e-8) + 0.1 * w
    return (w - 0.02 * step).astype(jnp.bfloat16), m, v


def clipped(gradients, sum_of_squares, count):
    factor = jnp.minimum(1.0, 0.5 * lax.rsqrt(sum_of_squares / count + 1e-30))
    return [g * factor for g in gradients]


def solution(mesh):
    def fetched(weights, number):
        return {name: lax.all_gather(w[number], "dp", axis=0, tiled=True) for name, w in zip(NAMES, weights, strict=True)}

    def step(x, dy, *arrays):
        weights, m, v = (arrays[i : i + 3] for i in (0, 3, 6))
        layers = weights[0].shape[0]
        h, kept = x[0], []
        for number in range(layers):
            kept.append(h)
            h = layer(h, fetched(weights, number))
        by_h, mine = dy[0], [None] * layers
        for number in reversed(range(layers)):
            _, back = jax.vjp(lambda w, h: layer(h, w), fetched(weights, number), kept[number])
            by_w, by_h = back(by_h)
            mine[number] = [lax.psum_scatter(by_w[name], "dp", scatter_dimension=0, tiled=True) for name in NAMES]
        gradients = [jnp.stack([mine[number][i] for number in range(layers)]).astype(jnp.float32) for i in range(3)]
        squares = lax.psum(sum(jnp.sum(g * g) for g in gradients), "dp")
        gradients = clipped(gradients, squares, lax.psum(1, "dp") * sum(g.size for g in gradients))
        new = [adamw(w.astype(jnp.float32), m, v, g) for w, m, v, g in zip(weights, m, v, gradients, strict=True)]
        return tuple(one[which] for which in range(3) for one in new)

    states, cut = P(("rep", "dp"), None, None), P(None, "dp", None)
    return jax.shard_map(
        step,
        mesh=mesh,
        in_specs=(states, states) + (cut,) * 9,
        out_specs=(P("rep", "dp", None),) * 9,
        check_vma=False,
    )
```

profile of v0, /device:TPU:0, one launch (start us, length us, event | category | flops | bytes accessed | tf_op | source)
XLA Modules:
  0.0 1205.0 jit_solution(16863950285541800999)
XLA Ops:
  7.2 2.7 fusion.104
  10.0 2.7 fusion.103
  12.7 2.6 fusion.102
  15.4 0.5 all-gather.21.cloned.1.call-update
  16.0 0.5 all-gather.23.cloned.1.call-update
  16.5 0.5 all-gather.19.cloned.1.call-update
  17.1 8.7 copy.20
  25.8 4.1 fusion.21
  30.0 8.7 copy.21
  38.7 37.3 %all-gather.13.cloned.1.call-done = bf16[1,1536,4096]{2,1,0:T(8,128)(2,1)} async-done(((bf16[1,96,4096]{2,1,0:T(8,128)(2,1)}), bf16[1,1536,4096]{2,1,0:T(8,128)(2,1)}) %all-gather.13.cloned.1.call-update) | async-done | bytes 12582928 | tf_op jit(solution)/shard_map/all_gather | solution.py:40
  75.9 34.2 %fusion.41 = f32[2048,4096]{1,0:T(8,128)} fusion(bf16[1,1536,4096]{2,1,0:T(8,128)(2,1)} %all-gather.13.cloned.1.call-done, bf16[1,2048,1536]{1,2,0:T(8,128)(2,1)} %copy.20, f32[2048]{0:T(1024)S(1)} %add_rsqrt_fusion), kind=kOutput, calls=%fused_computation.59 | convolution fusion | flops 25779240960 | bytes 52436992 | tf_op jit(solution)/shard_map/dot_general | solution.py:21
  110.1 30.9 %all-gather.15.cloned.1.call-done = bf16[1,1536,4096]{2,1,0:T(8,128)(2,1)} async-done(((bf16[1,96,4096]{2,1,0:T(8,128)(2,1)}), bf16[1,1536,4096]{2,1,0:T(8,128)(2,1)}) %all-gather.15.cloned.1.call-update) | async-done | bytes 12582928 | tf_op jit(solution)/shard_map/all_gather | solution.py:40
  141.1 43.9 %multiply_convert_fusion.1 = (bf16[2048,4096]{1,0:T(8,128)(2,1)}, f32[2048,4096]{1,0:T(8,128)}) fusion(f32[2048,4096]{1,0:T(8,128)} %fusion.41, bf16[1,1536,4096]{2,1,0:T(8,128)(2,1)} %all-gather.15.cloned.1.call-done, bf16[1,2048,1536]{1,2,0:T(8,128)(2,1)} %copy.20, f32[2048]{0:T(1024)S(1)} %add_rsqrt_fusion), kind=kOutput, calls=%fused_computation.17 | convolution fusion | flops 25829572608 | bytes 102768640 | tf_op jit(solution)/shard_map/dot_general | solution.py:22
  185.0 21.2 %all-gather.17.cloned.1.call-done = bf16[1,4096,1536]{2,1,0:T(8,128)(2,1)} async-done(((bf16[1,256,1536]{2,1,0:T(8,128)(2,1)}), bf16[1,4096,1536]{2,1,0:T(8,128)(2,1)}) %all-gather.17.cloned.1.call-update) | async-done | bytes 12582928 | tf_op jit(solution)/shard_map/all_gather | solution.py:40
  206.2 47.1 %fusion.25 = (f32[2048]{0:T(1024)S(1)}, bf16[2048,1536]{0,1:T(8,128)(2,1)}) fusion(bf16[2048,4096]{1,0:T(8,128)(2,1)} %get-tuple-element.24, bf16[1,4096,1536]{2,1,0:T(8,128)(2,1)} %all-gather.17.cloned.1.call-done, bf16[1,2048,1536]{1,2,0:T(8,128)(2,1)} %copy.20), kind=kOutput, calls=%fused_computation.43 | convolution fusion | flops 25785530368 | bytes 41951232 | tf_op jit(solution)/shard_map/dot_general | solution.py:10
  253.3 0.6 copy-done.14
  253.9 17.3 %all-gather.21.cloned.1.call-done = bf16[1,4096,1536]{2,1,0:T(8,128)(2,1)} async-done(((bf16[1,256,1536]{2,1,0:T(8,128)(2,1)}), bf16[1,4096,1536]{2,1,0:T(8,128)(2,1)}) %all-gather.21.cloned.1.call-update) | async-done | bytes 12582928 | tf_op jit(solution)/shard_map/all_gather | solution.py:40
  271.2 32.8 %convolution_convert_fusion.3 = bf16[2048,4096]{1,0:T(8,128)(2,1)} fusion(bf16[1,4096,1536]{2,1,0:T(8,128)(2,1)} %all-gather.21.cloned.1.call-done, bf16[1,2048,1536]{2,1,0:T(8,128)(2,1)} %param.12), kind=kOutput, calls=%fused_computation.38 | convolution fusion | flops 25778192384 | bytes 35651584 | tf_op jit(solution)/shard_map/transpose(jvp())/dot_general | solution.py:10
  304.0 32.2 %all-gather.23.cloned.1.call-done = bf16[1,1536,4096]{2,1,0:T(8,128)(2,1)} async-done(((bf16[1,96,4096]{2,1,0:T(8,128)(2,1)}), bf16[1,1536,4096]{2,1,0:T(8,128)(2,1)}) %all-gather.23.cloned.1.call-update) | async-done | bytes 12582928 | tf_op jit(solution)/shard_map/all_gather | solution.py:40
  336.2 34.3 %fusion.28 = f32[2048,4096]{1,0:T(8,128)} fusion(bf16[1,1536,4096]{2,1,0:T(8,128)(2,1)} %all-gather.23.cloned.1.call-done, bf16[2048,1536]{0,1:T(8,128)(2,1)} %get-tuple-element.27, f32[2048]{0:T(1024)S(1)} %fusion.90), kind=kOutput, calls=%fused_computation.46 | convolution fusion | flops 25779240960 | bytes 52436992 | tf_op jit(solution)/shard_map/jvp()/dot_general | solution.py:22
  370.5 30.6 %all-gather.19.cloned.1.call-done = bf16[1,1536,4096]{2,1,0:T(8,128)(2,1)} async-done(((bf16[1,96,4096]{2,1,0:T(8,128)(2,1)}), bf16[1,1536,4096]{2,1,0:T(8,128)(2,1)}) %all-gather.19.cloned.1.call-update) | async-done | bytes 12582928 | tf_op jit(solution)/shard_map/all_gather | solution.py:40
  401.2 55.3 %fusion.2 = (bf16[2048,4096]{1,0:T(8,128)(2,1)}, f32[2048,4096]{1,0:T(8,128)}) fusion(f32[2048,4096]{1,0:T(8,128)} %fusion.28, bf16[2048,4096]{1,0:T(8,128)(2,1)} %convolution_convert_fusion.3, bf16[1,1536,4096]{2,1,0:T(8,128)(2,1)} %all-gather.19.cloned.1.call-done, bf16[2048,1536]{0,1:T(8,128)(2,1)} %get-tuple-element.27, f32[2048]{0:T(1024)S(1)} %fusion.90), kind=kOutput, calls=%fused_computation.8 | convolution fusion | flops 25879904256 | bytes 119545856 | tf_op jit(solution)/shard_map/jvp()/dot_general | solution.py:21
  456.4 34.2 %fusion.46 = bf16[2048,1536]{0,1:T(8,128)(2,1)} fusion(bf16[2048,4096]{1,0:T(8,128)(2,1)} %get-tuple-element.28, bf16[1,1536,4096]{2,1,0:T(8,128)(2,1)} %all-gather.19.cloned.1.call-done), kind=kOutput, calls=%fused_computation.62 | convolution fusion | flops 25769803776 | bytes 35651584 | tf_op jit(solution)/shard_map/transpose(jvp())/dot_general | solution.py:21
  490.7 42.9 %fusion.27 = (f32[2048]{0:T(1024)S(1)}, bf16[2048,1536]{0,1:T(8,128)(2,1)}) fusion(bf16[2048,1536]{0,1:T(8,128)(2,1)} %get-tuple-element.27, bf16[2048,1536]{0,1:T(8,128)(2,1)} %fusion.46, bf16[1,1536,4096]{2,1,0:T(8,128)(2,1)} %all-gather.23.cloned.1.call-done, bf16[2048,4096]{1,0:T(8,128)(2,1)} %convolution_convert_fusion.3, ...), kind=kOutput, calls=%fused_computation.45 | convolution fusion | flops 25839007744 | bytes 81797120 | tf_op jit(solution)/shard_map/transpose(jvp())/dot_general | solution.py:22
  533.5 8.6 fusion.52
  542.2 2.8 copy-done.2
  545.0 31.3 %convolution_convert_fusion.1 = bf16[4096,1536]{1,0:T(8,128)(2,1)} fusion(bf16[2048,4096]{1,0:T(8,128)(2,1)} %get-tuple-element.24, bf16[2048,1536]{0,1:T(8,128)(2,1)S(1)} %fusion.52), kind=kOutput, calls=%fused_computation.33 | convolution fusion | flops 25776095232 | bytes 35651584 | tf_op jit(solution)/shard_map/transpose(jvp())/dot_general | solution.py:10
  576.3 38.2 %fusion.15 = bf16[4096,1536]{1,0:T(8,128)(2,1)} fusion(f32[2048,4096]{1,0:T(8,128)} %fusion.28, bf16[1,2048,1536]{2,1,0:T(8,128)(2,1)} %param.12, f32[2048,4096]{1,0:T(8,128)} %get-tuple-element.29), kind=kOutput, calls=%fused_computation.32 | convolution fusion | flops 25826426880 | bytes 85983232 | tf_op jit(solution)/shard_map/transpose(jvp())/dot_general | solution.py:10
  614.6 33.5 %convolution_convert_fusion.2 = bf16[2048,4096]{1,0:T(8,128)(2,1)} fusion(bf16[2048,1536]{0,1:T(8,128)(2,1)} %copy-done.2, bf16[1,4096,1536]{2,1,0:T(8,128)(2,1)} %all-gather.17.cloned.1.call-done), kind=kOutput, calls=%fused_computation.37 | convolution fusion | flops 25778192384 | bytes 35651584 | tf_op jit(solution)/shard_map/transpose(jvp())/dot_general | solution.py:10
  648.1 35.9 %fusion.20 = bf16[1536,4096]{1,0:T(8,128)(2,1)} fusion(bf16[2048,4096]{1,0:T(8,128)(2,1)} %convolution_convert_fusion.2, f32[2048,4096]{1,0:T(8,128)} %fusion.41, bf16[1,2048,1536]{1,2,0:T(8,128)(2,1)} %copy.20, f32[2048]{0:T(1024)S(1)} %copy-done.17), kind=kOutput, calls=%fused_computation.36 | convolution fusion | flops 25835864064 | bytes 69214208 | tf_op jit(solution)/shard_map/transpose(jvp())/dot_general | solution.py:22
  684.1 0.6 copy-done.13
  684.7 35.8 %fusion.16 = bf16[1536,4096]{1,0:T(8,128)(2,1)} fusion(bf16[2048,4096]{1,0:T(8,128)(2,1)} %convolution_convert_fusion.3, bf16[2048,1536]{0,1:T(8,128)(2,1)} %get-tuple-element.27, f32[2048]{0:T(1024)S(1)} %copy-done.13, f32[2048,4096]{1,0:T(8,128)} %get-tuple-element.29), kind=kOutput, calls=%fused_computation.34 | convolution fusion | flops 25835864064 | bytes 69214208 | tf_op jit(solution)/shard_map/transpose(jvp())/dot_general | solution.py:22
  720.6 41.2 %fusion.17 = bf16[1536,4096]{1,0:T(8,128)(2,1)} fusion(f32[2048,4096]{1,0:T(8,128)} %fusion.41, f32[2048,4096]{1,0:T(8,128)} %get-tuple-element.25, bf16[2048,4096]{1,0:T(8,128)(2,1)} %convolution_convert_fusion.2, bf16[1,2048,1536]{1,2,0:T(8,128)(2,1)} %copy.20, f32[2048]{0:T(1024)S(1)} %copy-done.17), kind=kOutput, calls=%fused_computation.35 | convolution fusion | flops 25877807104 | bytes 102768640 | tf_op jit(solution)/shard_map/transpose(jvp())/dot_general | solution.py:21
  761.8 32.9 %convolution_convert_fusion = bf16[1536,4096]{1,0:T(8,128)(2,1)} fusion(bf16[2048,4096]{1,0:T(8,128)(2,1)} %get-tuple-element.28, bf16[2048,1536]{0,1:T(8,128)(2,1)} %get-tuple-element.27, f32[2048]{0:T(1024)S(1)} %copy-done.13), kind=kOutput, calls=%fused_computation.31 | convolution fusion | flops 25779240960 | bytes 35659776 | tf_op jit(solution)/shard_map/transpose(jvp())/dot_general | solution.py:21
  794.9 2.9 fusion.80
  797.8 59.2 %reduce-scatter.11.cloned.1.call-done = bf16[96,4096]{1,0:T(8,128)(2,1)} async-done(((bf16[1536,4096]{1,0:T(8,128)(2,1)}), bf16[96,4096]{1,0:T(8,128)(2,1)}) %reduce-scatter.11.cloned.1.call-update) | async-done | bytes 786448 | tf_op jit(solution)/shard_map/reduce_scatter | solution.py:53
  857.0 94.9 %reduce-scatter.13.cloned.1.call-done = bf16[96,4096]{1,0:T(8,128)(2,1)} async-done(((bf16[1536,4096]{1,0:T(8,128)(2,1)}), bf16[96,4096]{1,0:T(8,128)(2,1)}) %reduce-scatter.13.cloned.1.call-update) | async-done | bytes 786448 | tf_op jit(solution)/shard_map/reduce_scatter | solution.py:53
  952.0 2.8 fusion.79
  954.8 92.3 %reduce-scatter.7.cloned.1.call-done = bf16[96,4096]{1,0:T(8,128)(2,1)} async-done(((bf16[1536,4096]{1,0:T(8,128)(2,1)}), bf16[96,4096]{1,0:T(8,128)(2,1)}) %reduce-scatter.7.cloned.1.call-update) | async-done | bytes 786448 | tf_op jit(solution)/shard_map/reduce_scatter | solution.py:53
  1047.1 95.0 %reduce-scatter.9.cloned.1.call-done = bf16[96,4096]{1,0:T(8,128)(2,1)} async-done(((bf16[1536,4096]{1,0:T(8,128)(2,1)}), bf16[96,4096]{1,0:T(8,128)(2,1)}) %reduce-scatter.9.cloned.1.call-update) | async-done | bytes 786448 | tf_op jit(solution)/shard_map/reduce_scatter | solution.py:53
  1142.0 2.8 fusion.78
  1146.8 31.8 %psum.7 = f32[]{:T(128)} all-reduce(f32[]{:T(128)S(6)} %add.99), channel_id=1, replica_groups=mesh['rep'=1,'dp'=16] {'dp'}, use_global_device_ids=true, to_apply=%region_12.13 | all-reduce | flops 1 | bytes 8 | tf_op jit(solution)/shard_map/psum | solution.py:55
  1179.4 7.3 fusion.86
  1186.8 0.9 copy-done.4
  1187.7 1.0 copy-done.5
  1188.6 0.9 copy-done.6
  1189.6 0.2 copy-done.8
  1190.3 7.3 fusion.77
  (55 shorter events, 1.3 us)
Async XLA Ops:
  7.2 68.8 %all-gather.13.cloned.1.call-start = ((), (), s32[]{:S(2)}) async-start(), calls=%async_computation.12 | async-start | bytes 13369344 | tf_op jit(solution)/shard_map/all_gather | solution.py:40
  9.9 131.2 %all-gather.15.cloned.1.call-start = ((), (), s32[]{:S(2)}) async-start(), calls=%async_computation.13 | async-start | bytes 13369344 | tf_op jit(solution)/shard_map/all_gather | solution.py:40
  12.6 193.6 %all-gather.17.cloned.1.call-start = ((), (), s32[]{:S(2)}) async-start(), calls=%async_computation.14 | async-start | bytes 13369344 | tf_op jit(solution)/shard_map/all_gather | solution.py:40
  15.3 255.9 %all-gather.21.cloned.1.call-start = ((), (), s32[]{:S(2)}) async-start(), calls=%async_computation.16 | async-start | bytes 13369344 | tf_op jit(solution)/shard_map/all_gather | solution.py:40
  15.9 320.3 %all-gather.23.cloned.1.call-start = ((), (), s32[]{:S(2)}) async-start(), calls=%async_computation.17 | async-start | bytes 13369344 | tf_op jit(solution)/shard_map/all_gather | solution.py:40
  16.5 384.7 %all-gather.19.cloned.1.call-start = ((), (), s32[]{:S(2)}) async-start(), calls=%async_computation.15 | async-start | bytes 13369344 | tf_op jit(solution)/shard_map/all_gather | solution.py:40
  17.1 777.7 %reduce-scatter.15.cloned.1.call-start = ((), (), s32[]{:S(2)}) async-start(), calls=%async_computation.10 | async-start | bytes 13369344 | tf_op jit(solution)/shard_map/reduce_scatter | solution.py:53
  30.0 111.1 %copy-start.16 = (f32[2048]{0:T(1024)}, f32[2048]{0:T(1024)S(1)}, u32[]{:S(2)}) copy-start(f32[2048]{0:T(1024)S(1)} %add_rsqrt_fusion) | copy-start | bytes 24580
  253.3 0.6 copy-start.14
  253.9 147.3 %copy-start.11 = (f32[2048]{0:T(1024)}, f32[2048]{0:T(1024)S(1)}, u32[]{:S(2)}) copy-start(f32[2048]{0:T(1024)S(1)} %fusion.90) | copy-start | bytes 24580
  490.7 42.9 %copy-start.15 = (f32[2048]{0:T(1024)S(1)}, f32[2048]{0:T(1024)}, u32[]{:S(2)}) copy-start(f32[2048]{0:T(1024)} %copy-done.14) | copy-start | bytes 24580
  490.7 42.9 %copy-start.12 = (f32[2048]{0:T(1024)S(1)}, f32[2048]{0:T(1024)}, u32[]{:S(2)}) copy-start(f32[2048]{0:T(1024)} %copy-done.11) | copy-start | bytes 24580
  542.2 2.8 copy-start.2
  576.2 218.6 %reduce-scatter.17.cloned.1.call-start = ((), (), s32[]{:S(2)}) async-start(), calls=%async_computation.11 | async-start | bytes 13369344 | tf_op jit(solution)/shard_map/reduce_scatter | solution.py:53
  614.5 33.6 %copy-start.17 = (f32[2048]{0:T(1024)S(1)}, f32[2048]{0:T(1024)}, u32[]{:S(2)}) copy-start(f32[2048]{0:T(1024)} %copy-done.16) | copy-start | bytes 24580
  614.5 242.5 %reduce-scatter.11.cloned.1.call-start = ((), (), s32[]{:S(2)}) async-start(), calls=%async_computation.8 | async-start | bytes 13369344 | tf_op jit(solution)/shard_map/reduce_scatter | solution.py:53
  684.0 0.7 copy-start.13
  684.0 267.9 %reduce-scatter.13.cloned.1.call-start = ((), (), s32[]{:S(2)}) async-start(), calls=%async_computation.9 | async-start | bytes 13369344 | tf_op jit(solution)/shard_map/reduce_scatter | solution.py:53
  720.5 326.6 %reduce-scatter.7.cloned.1.call-start = ((), (), s32[]{:S(2)}) async-start(), calls=%async_computation.6 | async-start | bytes 13369344 | tf_op jit(solution)/shard_map/reduce_scatter | solution.py:53
  761.8 380.3 %reduce-scatter.9.cloned.1.call-start = ((), (), s32[]{:S(2)}) async-start(), calls=%async_computation.7 | async-start | bytes 13369344 | tf_op jit(solution)/shard_map/reduce_scatter | solution.py:53
  794.8 392.0 %copy-start = (bf16[2,96,4096]{2,1,0:T(8,128)(2,1)S(1)}, bf16[2,96,4096]{2,1,0:T(8,128)(2,1)}, u32[]{:S(2)}) copy-start(bf16[2,96,4096]{2,1,0:T(8,128)(2,1)} %param.13) | copy-start | bytes 4718596
  794.8 392.0 %copy-start.1 = (bf16[2,96,4096]{2,1,0:T(8,128)(2,1)S(1)}, bf16[2,96,4096]{2,1,0:T(8,128)(2,1)}, u32[]{:S(2)}) copy-start(bf16[2,96,4096]{2,1,0:T(8,128)(2,1)} %param.14) | copy-start | bytes 4718596
  1179.3 7.4 copy-start.3
  1179.3 8.3 copy-start.4
  1179.3 9.3 copy-start.5
  1179.3 10.2 copy-start.6
  1179.4 10.3 copy-start.7
  1179.4 10.5 copy-start.8
  1179.4 10.7 copy-start.9
  1179.4 10.9 copy-start.10
Sparse Core Ops, SparseCore 0:
  10.8 65.1 all-gather.12
  78.7 62.2 all-gather.14
  143.9 62.2 all-gather.16
  208.9 62.2 all-gather.20
  273.8 62.2 all-gather.22
  338.8 62.2 all-gather.18
  576.4 90.4 reduce-scatter.14
  671.5 90.4 reduce-scatter.16
  766.6 90.4 reduce-scatter.10
  861.5 90.4 reduce-scatter.12
  956.6 90.4 reduce-scatter.6
  1051.6 90.4 reduce-scatter.8
where the time goes:
time: 1210 us; the launch traced here: 1200 us
  matrix products  573 us (47%)
  waiting for transfers between devices  513 us (42%)
  other arithmetic  36 us (3%)
  local copies, waits for them, and re-layouts  33 us (3%)
  blocking collectives  31.8 us (3%)
  between operations  17.5 us (1%)
    reduce_scatter x6, waiting for transfers between devices, step(): lax.psum_scatter(by_w[name], 'dp', scatter_dimension=0, tiled=True)  342 us
    dot_general x5, matrix products, layer(): gate = jnp.dot(a, w['w_gate'], preferred_element_type=jnp.float32)  198 us
    dot_general x5, matrix products, layer(): up = jnp.dot(a, w['w_up'], preferred_element_type=jnp.float32)  193 us
    dot_general x5, matrix products, matmul(): jnp.dot(a, w, preferred_element_type=jnp.float32).astype(jnp.bfloat16)  183 us
    all_gather x6, waiting for transfers between devices, fetched(): lax.all_gather(w[number], 'dp', axis=0, tiled=True)  170 us
    psum x1, blocking collectives, step(): squares = lax.psum(sum((jnp.sum(g * g) for g in gradients)), 'dp')  31.8 us
    unnamed x38, local copies, waits for them, and re-layouts  25 us
  transfers between devices with their start and end apart: 12, of which 10 were waited for; matrix products, arithmetic and copies ran while one was open for 37% of the time, Pallas kernels for 0%

commit v1 on v0

v1 whole, which is shorter than its diff:
```python
import functools

import jax
import jax.numpy as jnp
from jax import lax
from jax.experimental import pallas as pl
from jax.experimental.pallas import tpu as pltpu
from jax.sharding import PartitionSpec as P

NAMES = ("w_gate", "w_up", "w_down")
BF, F32 = jnp.bfloat16, jnp.float32
MESH = pl.DeviceIdType.MESH
TN = (((0,), (0,)), ((), ()))
NT = (((1,), (1,)), ((), ()))
M, D, F = 2048, 1536, 4096
UNITS = 48
OWN, IN = 10, 6
LAST = 5


def dot(a, b, dims):
    return lax.dot_general(a, b, dims, preferred_element_type=F32)


def matmul(a, w):
    return jnp.dot(a, w, preferred_element_type=F32).astype(BF)


def normed(h):
    wide = h.astype(F32)
    scale = lax.rsqrt(jnp.mean(wide**2, -1, keepdims=True) + 1e-6)
    return (wide * scale).astype(BF)


def adamw(w, m, v, g):
    m = 0.9 * m + 0.1 * g
    v = 0.95 * v + 0.05 * g * g
    step = m * lax.rsqrt(v + 1e-8) + 0.1 * w
    return (w - 0.02 * step).astype(BF), m, v


class Scatter:
    def __init__(self, own, r0, ra, rb, rc, sa, sb, sc, out, squares, sems, free, g_hbm):
        self.own, self.r0, self.ra, self.rb, self.rc = own, r0, ra, rb, rc
        self.sa, self.sb, self.sc, self.out, self.squares = sa, sb, sc, out, squares
        self.sems, self.free, self.g_hbm = sems, free, g_hbm
        me = lax.axis_index("dp")
        self.core, self.chip = me % 2, me // 2
        self.bits = ((me // 8) % 2, (me // 4) % 2, (me // 2) % 2)
        self.weights = (4, 2, 1)
        self.partner = me + 1 - 2 * self.core
        self.near = tuple(me + 2 * w * (1 - 2 * b) for b, w in zip(self.bits, self.weights, strict=True))

    def copy(self, phase, src, dst, slot, color, device):
        send, recv = self.sems[phase]
        at = (slot,) if color is None else (slot, color)
        return pltpu.make_async_remote_copy(
            src_ref=src, dst_ref=dst, send_sem=send.at[at], recv_sem=recv.at[at], device_id={"dp": device}, device_id_type=MESH
        )

    def copy_0(self, u):
        slot = lax.rem(u, IN)
        return self.copy(0, self.own.at[lax.rem(u, OWN), 1 - self.core], self.r0.at[slot], slot, None, self.partner)

    def copy_a(self, u, k):
        slot = lax.rem(u, IN)
        return self.copy(1, self.sa.at[slot, k], self.ra.at[slot, k], slot, k, self.near[k])

    def copy_b(self, u, k):
        slot = lax.rem(u, IN)
        return self.copy(2, self.sb.at[slot, k], self.rb.at[slot, k], slot, k, self.near[(k + 1) % 3])

    def copy_c(self, u, k):
        slot = lax.rem(u, IN)
        return self.copy(3, self.sc.at[slot, k], self.rc.at[slot, k], slot, k, self.near[(k + 2) % 3])

    def write(self, u):
        slot = lax.rem(u, IN)
        return pltpu.make_async_copy(self.out.at[slot], self.g_hbm.at[u], self.sems[4].at[slot])

    def index(self, k, a, b, c):
        return a * self.weights[k] + b * self.weights[(k + 1) % 3] + c * self.weights[(k + 2) % 3]

    def two(self, u, k, index):
        own = self.own[lax.rem(u, OWN), self.core, index, k].astype(F32)
        return own + self.r0[lax.rem(u, IN), index, k].astype(F32)

    def phase_0(self, u):
        @pl.when(u >= IN)
        def _():
            pl.semaphore_wait(self.free.at[3], 1)

        self.copy_0(u).start()

    def phase_a(self, u):
        @pl.when(u >= IN)
        def _():
            for axis in range(3):
                pl.semaphore_wait(self.free.at[axis], 1)

        self.copy_0(u).wait_recv()
        slot = lax.rem(u, IN)
        for k in range(3):
            away = 1 - self.bits[k]
            for b in range(2):
                for c in range(2):
                    self.sa[slot, k, 2 * b + c] = self.two(u, k, self.index(k, away, b, c)).astype(BF)
            self.copy_a(u, k).start()

    def phase_b(self, u):
        slot = lax.rem(u, IN)
        for k in range(3):
            here, away = self.bits[k], 1 - self.bits[(k + 1) % 3]
            self.copy_a(u, k).wait_recv()
            for c in range(2):
                total = self.two(u, k, self.index(k, here, away, c)) + self.ra[slot, k, 2 * away + c].astype(F32)
                self.sb[slot, k, c] = total.astype(BF)
            self.copy_b(u, k).start()

    def phase_c(self, u):
        slot = lax.rem(u, IN)
        for k in range(3):
            a, b, away = self.bits[k], self.bits[(k + 1) % 3], 1 - self.bits[(k + 2) % 3]
            self.copy_b(u, k).wait_recv()
            total = self.two(u, k, self.index(k, a, b, away)) + self.ra[slot, k, 2 * b + away].astype(F32)
            self.sc[slot, k] = (total + self.rb[slot, k, away].astype(F32)).astype(BF)
            self.copy_c(u, k).start()

    def phase_d(self, u):
        slot = lax.rem(u, IN)

        @pl.when(u >= IN)
        def _():
            self.write(u - IN).wait()

        for k in range(3):
            b, c = self.bits[(k + 1) % 3], self.bits[(k + 2) % 3]
            self.copy_c(u, k).wait_recv()
            total = self.two(u, k, self.chip) + self.ra[slot, k, 2 * b + c].astype(F32)
            total = total + self.rb[slot, k, c].astype(F32) + self.rc[slot, k].astype(F32)
            rounded = total.astype(BF)
            self.out[slot, pl.ds(32 * k, 32), :] = rounded
            wide = rounded.astype(F32)
            square = wide * wide
            self.squares[...] += square[0:8] + square[8:16] + square[16:24] + square[24:32]
        self.write(u).start()
        self.copy_0(u).wait_send()
        for k in range(3):
            self.copy_a(u, k).wait_send()
            self.copy_b(u, k).wait_send()
            self.copy_c(u, k).wait_send()

        @pl.when(u + IN < UNITS)
        def _():
            pl.semaphore_signal(self.free.at[3], inc=1, device_id={"dp": self.partner}, device_id_type=MESH)
            for axis in range(3):
                pl.semaphore_signal(self.free.at[axis], inc=1, device_id={"dp": self.near[axis]}, device_id_type=MESH)

    def tick(self, q, low, high):
        for lag, phase in ((LAST, self.phase_d), (4, self.phase_c), (3, self.phase_b), (1, self.phase_a), (0, self.phase_0)):
            u = q - lag

            @pl.when((u >= low) & (u < high))
            def _(phase=phase, u=u):
                phase(u)


class Plan:
    def __init__(self):
        self.first, self.low, self.made, self.log = LAST, 0, 0, []

    def stage(self, steps, per, of, units_after):
        ticks = [j // of * per + j % of for j in range(steps) if j % of < per]
        at = [j for j in range(steps) if j % of < per]
        stage = (self.first, self.low, self.made)
        for j in range(steps):
            if j in at:
                self.log.append((self.first + ticks[at.index(j)], self.low, self.made + units_after(j)))
            for u in range(self.made + units_after(j), self.made + units_after(j + 1)):
                assert u - OWN < self.low or u - OWN <= self.log[-1][0] - LAST, u
        self.first += len(ticks)
        self.made += units_after(steps)
        return stage

    def restart(self, idle):
        assert self.first - LAST >= self.made, (self.first, self.made)
        self.first, self.low = self.made - idle, self.made

    def check(self):
        seen = {}
        for q, low, high in self.log:
            for name, lag in (("d", LAST), ("c", 4), ("b", 3), ("a", 1), ("0", 0)):
                u = q - lag
                if low <= u < high:
                    seen.setdefault(u, []).append(name)
        assert all(seen.get(u) == ["0", "a", "b", "c", "d"] for u in range(UNITS)), seen


def backward_kernel(
    dy, act1, g1, u1, a1, h1, wd1, wg1, wu1, act0, g0, u0, a0, wd0,
    dg1, du1, dg0, du0, g_hbm, total_ref,
    x1, own, r0, ra, rb, rc, sa, sb, sc, out, squares, sums, sum_all,
    s0s, s0r, sas, sar, sbs, sbr, scs, scr, out_sem, free, sum_send, sum_recv, load_sem, act_sem,
):
    me = lax.axis_index("dp")
    barrier = pltpu.get_barrier_semaphore()
    for other in range(1, 16):
        pl.semaphore_signal(barrier, inc=1, device_id={"dp": (me + other) % 16}, device_id_type=MESH)
    pl.semaphore_wait(barrier, 15)

    sems = ((s0s, s0r), (sas, sar), (sbs, sbr), (scs, scr), out_sem)
    scatter = Scatter(own, r0, ra, rb, rc, sa, sb, sc, out, squares, sems, free, g_hbm)
    plan = Plan()
    squares[...] = jnp.zeros_like(squares)
    load = pltpu.make_async_copy(dy, x1, load_sem.at[0])
    load.start()

    def down_gradient(act, made, stage, ready):
        def body(held):
            def block(f):
                return pltpu.make_async_copy(act.at[:, pl.ds(pl.multiple_of(f * 512, 512), 512)], held.at[f], act_sem.at[f])

            for f in range(8):
                block(f).start()
            ready()

            def step(t, carry):
                columns, f = t // 8, lax.rem(t, 8)

                @pl.when(t < 8)
                def _():
                    block(f).wait()

                @pl.when(lax.rem(t, 5) == 0)
                def _():
                    scatter.tick(stage[0] + t // 5, stage[1], stage[2] + 2 * columns)

                tile = dot(held[f], x1[:, pl.ds(pl.multiple_of(columns * 384, 128), 384)], TN).astype(BF)
                for half in range(2):
                    slot = lax.rem(made + 2 * columns + half, OWN)
                    for core in range(2):
                        for k in range(3):
                            for q in range(4):
                                row = 256 * core + 128 * half + 32 * q
                                own[slot, core, f, k, :, 128 * q : 128 * q + 128] = tile[row : row + 32, 128 * k : 128 * k + 128]
                return carry

            lax.fori_loop(0, 32, step, 0)

        pl.run_scoped(body, pltpu.VMEM((8, M, 512), BF))

    def hidden(wd, g, u, dg, du, stage):
        def step(w_ref, g_ref, u_ref, dg_ref, du_ref):
            f, half = pl.program_id(0), pl.program_id(1)

            @pl.when(half == 0)
            def _():
                scatter.tick(stage[0] + f, stage[1], stage[2])

            for s in range(4):
                rows = pl.ds(256 * s, 256)
                by = dot(x1[pl.ds(pl.multiple_of(half * 1024, 1024) + 256 * s, 256), :], w_ref[...], NT).astype(BF).astype(F32)
                gate, up = g_ref[rows, :], u_ref[rows, :]
                sigmoid = lax.logistic(gate)
                silu = gate * sigmoid
                du_ref[rows, :] = (by * silu).astype(BF)
                dg_ref[rows, :] = (by * up * (sigmoid + silu * (1.0 - sigmoid))).astype(BF)

        tile = pl.BlockSpec((1024, 512), lambda f, half: (half, f))
        pltpu.emit_pipeline(
            step, grid=(8, 2), in_specs=[pl.BlockSpec((512, D), lambda f, half: (f, 0)), tile, tile], out_specs=[tile, tile]
        )(wd, g, u, dg, du)

    def wide_gradient(x2, by, made, stage, per):
        def step(by_ref):
            j = pl.program_id(0)

            @pl.when(lax.rem(j, 4) < per)
            def _():
                scatter.tick(stage[0] + j // 4 * per + lax.rem(j, 4), stage[1], stage[2] + j)

            slot = lax.rem(made + j, OWN)
            for b in range(4):
                tile = dot(x2[:, 384 * b : 384 * b + 384], by_ref[...], TN).astype(BF)
                for s in range(4):
                    for k in range(3):
                        row = 96 * s + 32 * k
                        own[slot, s % 2, 2 * b + s // 2, k, :, :] = tile[row : row + 32, :]

        pltpu.emit_pipeline(step, grid=(8,), in_specs=[pl.BlockSpec((M, 512), lambda j: (0, j))], out_specs=[])(by)

    def states(stage):
        def body(da, held):
            def step(dg_ref, du_ref, wg_ref, wu_ref):
                m, n = pl.program_id(0), pl.program_id(1)
                rows = pl.ds(pl.multiple_of(m * 512, 512), 512)
                take = pltpu.make_async_copy(h1.at[rows], held, load_sem.at[2])

                @pl.when(n == 0)
                def _():
                    take.start()

                @pl.when(lax.rem(n, 2) == 0)
                def _():
                    scatter.tick(stage[0] + 3 * m + n // 2, stage[1], stage[2])

                by_gate = dot(dg_ref[...], wg_ref[...], NT).astype(BF).astype(F32)
                by_up = dot(du_ref[...], wu_ref[...], NT).astype(BF).astype(F32)
                da[n] = (by_gate + by_up).astype(BF)

                @pl.when(n == 5)
                def _():
                    take.wait()

                    def some(i, carry):
                        at = pl.ds(pl.multiple_of(i * 32, 32), 32)
                        wide = held[at, :].astype(F32)
                        scale = lax.rsqrt(jnp.mean(wide * wide, -1, keepdims=True) + 1e-6)
                        by = jnp.concatenate([da[n, at, :] for n in range(6)], axis=-1).astype(F32)
                        inner = jnp.sum(by * wide, -1, keepdims=True)
                        back = (by * scale - wide * (inner * scale * scale * scale * (1.0 / D))).astype(BF)
                        at_all = pl.ds(pl.multiple_of(m * 512 + i * 32, 32), 32)
                        x1[at_all, :] = (x1[at_all, :].astype(F32) + back.astype(F32)).astype(BF)
                        return carry

                    lax.fori_loop(0, 16, some, 0)

            tile = pl.BlockSpec((512, F), lambda m, n: (m, 0))
            rows = pl.BlockSpec((256, F), lambda m, n: (n, 0))
            pltpu.emit_pipeline(step, grid=(4, 6), in_specs=[tile, tile, rows, rows], out_specs=[])(dg1, du1, wg1, wu1)

        pl.run_scoped(body, pltpu.VMEM((6, 512, 256), BF), pltpu.VMEM((512, D), BF))

    def later(x2):
        take = pltpu.make_async_copy(a1, x2, load_sem.at[1])
        take.start()
        plan.restart(2)
        stage = plan.stage(32, 1, 5, lambda t: 2 * (t // 8))
        down_gradient(act1, 0, stage, load.wait)
        stage = plan.stage(8, 1, 1, lambda j: 0)
        hidden(wd1, g1, u1, dg1, du1, stage)
        plan.restart(1)
        take.wait()
        stage = plan.stage(8, 3, 4, lambda j: j)
        wide_gradient(x2, dg1, 8, stage, 3)
        stage = plan.stage(8, 3, 4, lambda j: j)
        wide_gradient(x2, du1, 16, stage, 3)

    def sooner(x2):
        take = pltpu.make_async_copy(a0, x2, load_sem.at[1])
        take.start()
        plan.restart(2)
        stage = plan.stage(32, 1, 5, lambda t: 2 * (t // 8))
        down_gradient(act0, 24, stage, lambda: None)
        stage = plan.stage(8, 1, 1, lambda j: 0)
        hidden(wd0, g0, u0, dg0, du0, stage)
        plan.restart(1)
        take.wait()
        stage = plan.stage(8, 4, 4, lambda j: j)
        wide_gradient(x2, dg0, 32, stage, 4)
        stage = plan.stage(8, 4, 4, lambda j: j)
        wide_gradient(x2, du0, 40, stage, 4)

    pl.run_scoped(later, pltpu.VMEM((M, D), BF))
    stage = plan.stage(12, 1, 1, lambda j: 0)
    states(stage)
    pl.run_scoped(sooner, pltpu.VMEM((M, D), BF))
    left = UNITS + LAST - plan.first
    first, low, _ = plan.stage(left, 1, 1, lambda j: 0)
    plan.check()

    def rest(t, carry):
        scatter.tick(first + t, low, UNITS)
        return carry

    lax.fori_loop(0, left, rest, 0)
    for u in range(UNITS - IN, UNITS):
        scatter.write(u).wait()

    mine = jnp.sum(squares[...], axis=(0, 1), keepdims=True)
    sums[...] = jnp.broadcast_to(mine, sums.shape)

    def tell(to, of):
        return pltpu.make_async_remote_copy(
            src_ref=sums, dst_ref=sum_all.at[of], send_sem=sum_send.at[to], recv_sem=sum_recv.at[of], device_id={"dp": to}, device_id_type=MESH
        )

    for other in range(1, 16):
        tell((me + other) % 16, me).start()
    for other in range(1, 16):
        tell((me + other) % 16, (me + other) % 16).wait_recv()
    for other in range(1, 16):
        tell((me + other) % 16, me).wait_send()
    sum_all[me] = sums[...]
    total = sum_all[0]
    for i in range(1, 16):
        total = total + sum_all[i]
    total_ref[...] = total


def backward(*args):
    any_spec = pl.BlockSpec(memory_space=pl.ANY)
    shape = jax.ShapeDtypeStruct
    piece = (3, 32, 512)
    dma = pltpu.SemaphoreType.DMA
    outs = pl.pallas_call(
        backward_kernel,
        out_shape=[shape((M, F), BF)] * 4 + [shape((UNITS, 96, 512), BF), shape((8, 128), F32)],
        in_specs=[any_spec] * 14,
        out_specs=[any_spec] * 5 + [pl.BlockSpec(memory_space=pltpu.VMEM)],
        scratch_shapes=[
            pltpu.VMEM((M, D), BF),
            pltpu.VMEM((OWN, 2, 8, *piece), BF),
            pltpu.VMEM((IN, 8, *piece), BF),
            pltpu.VMEM((IN, 3, 4, 32, 512), BF),
            pltpu.VMEM((IN, 3, 2, 32, 512), BF),
            pltpu.VMEM((IN, *piece), BF),
            pltpu.VMEM((IN, 3, 4, 32, 512), BF),
            pltpu.VMEM((IN, 3, 2, 32, 512), BF),
            pltpu.VMEM((IN, *piece), BF),
            pltpu.VMEM((IN, 96, 512), BF),
            pltpu.VMEM((8, 512), F32),
            pltpu.VMEM((8, 128), F32),
            pltpu.VMEM((16, 8, 128), F32),
            dma((IN,)), dma((IN,)),
            dma((IN, 3)), dma((IN, 3)), dma((IN, 3)), dma((IN, 3)), dma((IN, 3)), dma((IN, 3)),
            dma((IN,)),
            pltpu.SemaphoreType.REGULAR((4,)),
            dma((16,)), dma((16,)), dma((3,)), dma((8,)),
        ],
        compiler_params=pltpu.CompilerParams(collective_id=0, has_side_effects=True, vmem_limit_bytes=67_000_000),
        cost_estimate=pl.CostEstimate(flops=10 * 2 * M * D * F, bytes_accessed=600_000_000, transcendentals=0),
        name="backward",
    )(*args)
    return outs[4], outs[5]


def solution(mesh):
    def fetched(weights, number):
        return {name: lax.all_gather(w[number], "dp", axis=0, tiled=True) for name, w in zip(NAMES, weights, strict=True)}

    def step(x, dy, *arrays):
        weights, m, v = (arrays[i : i + 3] for i in (0, 3, 6))
        h, kept = x[0], []
        for number in range(2):
            w = fetched(weights, number)
            a = normed(h)
            gate = jnp.dot(a, w["w_gate"], preferred_element_type=F32)
            up = jnp.dot(a, w["w_up"], preferred_element_type=F32)
            act = (jax.nn.silu(gate) * up).astype(BF)
            kept.append((h, a, gate, up, act, w))
            h = h + matmul(act, w["w_down"])
        (_, a0, g0, u0, act0, w0), (h1, a1, g1, u1, act1, w1) = kept
        units, total = backward(
            dy[0], act1, g1, u1, a1, h1, w1["w_down"], w1["w_gate"], w1["w_up"], act0, g0, u0, a0, w0["w_down"]
        )
        count = 16 * sum(w.size for w in weights)
        factor = jnp.minimum(1.0, 0.5 * lax.rsqrt(total[0, 0] / count + 1e-30))

        def wide(first):
            return units[first : first + 8].transpose(1, 0, 2).reshape(96, F)

        def down(first):
            return units[first : first + 8].reshape(4, 2, 3, 32, 4, 128).transpose(1, 4, 3, 0, 2, 5).reshape(256, D)

        gradients = [
            jnp.stack([wide(32), wide(8)]),
            jnp.stack([wide(40), wide(16)]),
            jnp.stack([down(24), down(0)]),
        ]
        gradients = [g.astype(F32) * factor for g in gradients]
        new = [adamw(w.astype(F32), m, v, g) for w, m, v, g in zip(weights, m, v, gradients, strict=True)]
        return tuple(one[which] for which in range(3) for one in new)

    states, cut = P(("rep", "dp"), None, None), P(None, "dp", None)
    return jax.shard_map(
        step,
        mesh=mesh,
        in_specs=(states, states) + (cut,) * 9,
        out_specs=(P("rep", "dp", None),) * 9,
        check_vma=False,
    )
```

time: 1210 us -> 908 us (0.75)
  Pallas kernels: 0 us -> 452 us
  matrix products: 573 us -> 186 us
  waiting for transfers between devices: 513 us -> 185 us
  blocking collectives: 31.8 us -> 0 us
    pallas_call x0 -> x1, Pallas kernels: none -> 452 us  [backward(): pl.pallas_call(backward_kernel, out_shape=[shape((M, F), BF)] * 4 + [shap...]
    dot_general x15 -> x5, matrix products: 573 us -> 186 us  [the longest x2 83.7 us: step(): up = jnp.dot(a, w['w_up'], preferred_element_type=F32)]
    reduce_scatter x6 -> x0, waiting for transfers between devices: 342 us -> none  [step(): lax.psum_scatter(by_w[name], 'dp', scatter_dimension=0, tiled=True)]
    psum x1 -> x0, blocking collectives: 31.8 us -> none  [step(): squares = lax.psum(sum((jnp.sum(g * g) for g in gradients)), 'dp')]
    unnamed x38 -> x24, local copies, waits for them, and re-layouts: 25 us -> 6.78 us
    all_gather x6, waiting for transfers between devices: 170 us -> 184 us  [fetched(): lax.all_gather(w[number], 'dp', axis=0, tiled=True)]
    convert_element_type x2 -> x4, other arithmetic: 14.7 us -> 25.5 us  [the longest x2 15.3 us: adamw(): return ((w - 0.02 * step).astype(BF), m, v)]
  transfers between devices with their start and end apart: 12 -> 6, of which waited for: 10 -> 6; matrix products, arithmetic and copies ran while one was open for 37% -> 22% of each run, Pallas kernels for 0% -> 0%
where the time goes in v1:
time: 908 us; the launch traced here: 905 us
  Pallas kernels  452 us (50%)
  matrix products  186 us (20%)
  waiting for transfers between devices  185 us (20%)
  local copies, waits for them, and re-layouts  36.1 us (4%)
  other arithmetic  29.6 us (3%)
  between operations  15.2 us (2%)
    pallas_call x1, Pallas kernels, backward(): pl.pallas_call(backward_kernel, out_shape=[shape((M, F), BF)] * 4 + [shap...  452 us
    all_gather x6, waiting for transfers between devices, fetched(): lax.all_gather(w[number], 'dp', axis=0, tiled=True)  184 us
    dot_general x2, matrix products, step(): up = jnp.dot(a, w['w_up'], preferred_element_type=F32)  83.7 us
    dot_general x2, matrix products, step(): gate = jnp.dot(a, w['w_gate'], preferred_element_type=F32)  68.3 us
    dot_general x1, matrix products, matmul(): return jnp.dot(a, w, preferred_element_type=F32).astype(BF)  33.6 us
  transfers between devices with their start and end apart: 6, of which 6 were waited for; matrix products, arithmetic and copies ran while one was open for 22% of the time, Pallas kernels for 0%

profile of v1, /device:TPU:0, one launch (start us, length us, event | category | flops | bytes accessed | tf_op | source)
XLA Modules:
  0.0 904.5 jit_solution(17548794268185290318)
XLA Ops:
  7.2 2.8 fusion.31
  10.0 0.0 all-gather.15.cloned.1.call-start
  10.1 1.2 fusion.32
  11.4 0.0 all-gather.17.cloned.1.call-start
  11.4 0.6 copy-done.3
  12.0 1.2 fusion.30
  13.3 0.5 all-gather.19.cloned.1.call-update
  13.9 0.5 all-gather.21.cloned.1.call-update
  14.5 0.5 all-gather.23.cloned.1.call-update
  15.0 4.1 fusion
  19.1 6.5 fusion.1.a0
  25.6 50.4 %all-gather.13.cloned.1.call-done = bf16[1,1536,4096]{2,1,0:T(8,128)(2,1)} async-done(((bf16[1,96,4096]{2,1,0:T(8,128)(2,1)}), bf16[1,1536,4096]{2,1,0:T(8,128)(2,1)}) %all-gather.13.cloned.1.call-update) | async-done | bytes 12582928 | tf_op jit(solution)/shard_map/all_gather | solution.py:440
  76.0 34.4 %fusion.6.g0 = f32[2048,4096]{1,0:T(8,128)} fusion(bf16[2048,1536]{1,0:T(8,128)(2,1)} %fusion.1.a0, bf16[1,1536,4096]{2,1,0:T(8,128)(2,1)} %all-gather.13.cloned.1.call-done), kind=kOutput, calls=%fused_computation.12 | convolution fusion | flops 25769803776 | bytes 52428800 | tf_op jit(solution)/shard_map/dot_general | solution.py:448
  110.3 30.8 %all-gather.15.cloned.1.call-done = bf16[1,1536,4096]{2,1,0:T(8,128)(2,1)} async-done(((bf16[1,96,4096]{2,1,0:T(8,128)(2,1)}), bf16[1,1536,4096]{2,1,0:T(8,128)(2,1)}) %all-gather.15.cloned.1.call-update) | async-done | bytes 12582928 | tf_op jit(solution)/shard_map/all_gather | solution.py:440
  141.1 41.9 %multiply_convert_fusion.1 = (bf16[2048,4096]{1,0:T(8,128)(2,1)}, f32[2048,4096]{1,0:T(8,128)}) fusion(f32[2048,4096]{1,0:T(8,128)} %fusion.6.g0, bf16[2048,1536]{1,0:T(8,128)(2,1)} %fusion.1.a0, bf16[1,1536,4096]{2,1,0:T(8,128)(2,1)} %all-gather.15.cloned.1.call-done), kind=kOutput, calls=%fused_computation.1 | convolution fusion | flops 25820135424 | bytes 102760448 | tf_op jit(solution)/shard_map/dot_general | solution.py:449
  182.9 23.3 %all-gather.17.cloned.1.call-done = bf16[1,4096,1536]{2,1,0:T(8,128)(2,1)} async-done(((bf16[1,256,1536]{2,1,0:T(8,128)(2,1)}), bf16[1,4096,1536]{2,1,0:T(8,128)(2,1)}) %all-gather.17.cloned.1.call-update) | async-done | bytes 12582928 | tf_op jit(solution)/shard_map/all_gather | solution.py:440
  206.2 33.6 %fusion.2 = (f32[2048]{0:T(1024)S(1)}, bf16[2048,1536]{1,0:T(8,128)(2,1)S(1)}) fusion(bf16[2048,4096]{1,0:T(8,128)(2,1)} %get-tuple-element.34.act0, bf16[1,4096,1536]{2,1,0:T(8,128)(2,1)} %all-gather.17.cloned.1.call-done, bf16[1,2048,1536]{2,1,0:T(8,128)(2,1)} %param.11), kind=kOutput, calls=%fused_computation.8 | convolution fusion | flops 25785530368 | bytes 41951232 | tf_op jit(solution)/shard_map/dot_general | solution.py:26
  239.9 2.6 copy-done.5
  242.5 3.7 fusion.3.a1
  246.2 25.0 %all-gather.19.cloned.1.call-done = bf16[1,1536,4096]{2,1,0:T(8,128)(2,1)} async-done(((bf16[1,96,4096]{2,1,0:T(8,128)(2,1)}), bf16[1,1536,4096]{2,1,0:T(8,128)(2,1)}) %all-gather.19.cloned.1.call-update) | async-done | bytes 12582928 | tf_op jit(solution)/shard_map/all_gather | solution.py:440
  271.2 34.0 %fusion.23.g1 = f32[2048,4096]{1,0:T(8,128)} fusion(bf16[2048,1536]{1,0:T(8,128)(2,1)} %fusion.3.a1, bf16[1,1536,4096]{2,1,0:T(8,128)(2,1)} %all-gather.19.cloned.1.call-done), kind=kOutput, calls=%fused_computation.56 | convolution fusion | flops 25769803776 | bytes 52428800 | tf_op jit(solution)/shard_map/dot_general | solution.py:448
  305.2 31.0 %all-gather.21.cloned.1.call-done = bf16[1,1536,4096]{2,1,0:T(8,128)(2,1)} async-done(((bf16[1,96,4096]{2,1,0:T(8,128)(2,1)}), bf16[1,1536,4096]{2,1,0:T(8,128)(2,1)}) %all-gather.21.cloned.1.call-update) | async-done | bytes 12582928 | tf_op jit(solution)/shard_map/all_gather | solution.py:440
  336.2 41.8 %multiply_convert_fusion = (bf16[2048,4096]{1,0:T(8,128)(2,1)}, f32[2048,4096]{1,0:T(8,128)}) fusion(f32[2048,4096]{1,0:T(8,128)} %fusion.23.g1, bf16[2048,1536]{1,0:T(8,128)(2,1)} %fusion.3.a1, bf16[1,1536,4096]{2,1,0:T(8,128)(2,1)} %all-gather.21.cloned.1.call-done), kind=kOutput, calls=%fused_computation | convolution fusion | flops 25820135424 | bytes 102760448 | tf_op jit(solution)/shard_map/dot_general | solution.py:449
  378.0 23.2 %all-gather.23.cloned.1.call-done = bf16[1,4096,1536]{2,1,0:T(8,128)(2,1)} async-done(((bf16[1,256,1536]{2,1,0:T(8,128)(2,1)}), bf16[1,4096,1536]{2,1,0:T(8,128)(2,1)}) %all-gather.23.cloned.1.call-update) | async-done | bytes 12582928 | tf_op jit(solution)/shard_map/all_gather | solution.py:440
  401.2 452.5 %backward.1 = (bf16[2048,4096]{1,0:T(8,128)(2,1)}, bf16[2048,4096]{1,0:T(8,128)(2,1)}, bf16[2048,4096]{1,0:T(8,128)(2,1)}, bf16[2048,4096]{1,0:T(8,128)(2,1)}, b...) custom-call(bf16[2048,1536]{1,0:T(8,128)(2,1)} %bitcast.53, bf16[2048,4096]{1,0:T(8,128)(2,1)} %get-tuple-element.38.act1, ...), custom_call_target="tpu_custom_call" | custom-call | flops 257698037760 | bytes 600000000 | tf_op jit(solution)/shard_map/backward/pallas_call | solution.py:406
  853.6 1.2 slice.47
  855.5 3.9 fusion.29
  859.4 1.1 reshape.47
  860.4 1.8 copy.34
  862.3 0.7 stack_reshape.22
  863.0 0.2 reshape.48
  863.2 0.7 copy.33
  863.8 0.7 stack_reshape.23
  864.6 1.6 copy.27
  866.1 1.2 stack_reshape.21
  867.4 0.4 copy.26
  867.8 1.2 stack_reshape.20
  869.0 2.6 copy.25
  871.6 2.2 stack_reshape.19
  873.8 2.4 copy.24
  876.3 2.2 stack_reshape.18
  878.6 6.9 fusion.17
  885.4 1.4 copy-done.7
  886.9 0.9 copy-done.8
  887.8 0.9 copy-done.9
  888.7 0.1 copy-done.10
  888.8 0.2 copy-done.11
  889.0 8.5 fusion.11
  (26 shorter events, 0.3 us)
Async XLA Ops:
  7.2 2.9 copy-start.1
  7.2 68.8 %all-gather.13.cloned.1.call-start = ((), (), s32[]{:S(2)}) async-start(), calls=%async_computation | async-start | bytes 13369344 | tf_op jit(solution)/shard_map/all_gather | solution.py:440
  10.0 2.0 copy-start.3
  10.0 131.0 %all-gather.15.cloned.1.call-start = ((), (), s32[]{:S(2)}) async-start(), calls=%async_computation.1 | async-start | bytes 13369344 | tf_op jit(solution)/shard_map/all_gather | solution.py:440
  11.4 194.9 %all-gather.17.cloned.1.call-start = ((), (), s32[]{:S(2)}) async-start(), calls=%async_computation.2 | async-start | bytes 13369344 | tf_op jit(solution)/shard_map/all_gather | solution.py:440
  13.2 257.9 %all-gather.19.cloned.1.call-start = ((), (), s32[]{:S(2)}) async-start(), calls=%async_computation.3 | async-start | bytes 13369344 | tf_op jit(solution)/shard_map/all_gather | solution.py:440
  13.8 322.3 %all-gather.21.cloned.1.call-start = ((), (), s32[]{:S(2)}) async-start(), calls=%async_computation.4 | async-start | bytes 13369344 | tf_op jit(solution)/shard_map/all_gather | solution.py:440
  14.4 386.7 %all-gather.23.cloned.1.call-start = ((), (), s32[]{:S(2)}) async-start(), calls=%async_computation.5 | async-start | bytes 13369344 | tf_op jit(solution)/shard_map/all_gather | solution.py:440
  239.9 2.6 copy-start.5
  869.0 9.4 %copy-start.4 = (bf16[2,256,1536]{2,1,0:T(8,128)(2,1)S(1)}, bf16[2,256,1536]{2,1,0:T(8,128)(2,1)}, u32[]{:S(2)}) copy-start(bf16[2,256,1536]{2,1,0:T(8,128)(2,1)} %param.15) | copy-start | bytes 4718596
  878.5 7.0 copy-start
  878.5 7.0 copy-start.2
  878.5 7.0 copy-start.6
  878.5 8.4 copy-start.7
  878.5 9.3 %copy-start.8 = (f32[2,96,4096]{2,1,0:T(8,128)S(1)}, f32[2,96,4096]{2,1,0:T(8,128)}, u32[]{:S(2)}) copy-start(f32[2,96,4096]{2,1,0:T(8,128)} %param.20) | copy-start | bytes 9437188
  878.5 10.2 %copy-start.9 = (f32[2,96,4096]{2,1,0:T(8,128)S(1)}, f32[2,96,4096]{2,1,0:T(8,128)}, u32[]{:S(2)}) copy-start(f32[2,96,4096]{2,1,0:T(8,128)} %param.17) | copy-start | bytes 9437188
  878.5 10.3 %copy-start.10 = (bf16[1,96,4096]{2,1,0:T(8,128)(2,1)S(1)}, bf16[1,96,4096]{2,1,0:T(8,128)(2,1)}, u32[]{:S(2)}) copy-start(bf16[1,96,4096]{2,1,0:T(8,128)(2,1)} %stack_reshape.21) | copy-start | bytes 2359300
  878.5 10.5 %copy-start.11 = (bf16[1,96,4096]{2,1,0:T(8,128)(2,1)S(1)}, bf16[1,96,4096]{2,1,0:T(8,128)(2,1)}, u32[]{:S(2)}) copy-start(bf16[1,96,4096]{2,1,0:T(8,128)(2,1)} %stack_reshape.20) | copy-start | bytes 2359300
Sparse Core Ops, SparseCore 0:
  10.8 65.1 all-gather.12
  78.7 62.2 all-gather.14
  143.9 62.2 all-gather.16
  208.9 62.2 all-gather.18
  273.8 62.2 all-gather.20
  338.8 62.2 all-gather.22

commit v2 on v0

v2 whole, which is shorter than its diff:
```python
import functools

import jax
import jax.numpy as jnp
from jax import lax
from jax.experimental import pallas as pl
from jax.experimental.pallas import tpu as pltpu
from jax.sharding import PartitionSpec as P

NAMES = ("w_gate", "w_up", "w_down")
BF, F32 = jnp.bfloat16, jnp.float32
MESH = pl.DeviceIdType.MESH
TN = (((0,), (0,)), ((), ()))
NT = (((1,), (1,)), ((), ()))
M, D, F = 2048, 1536, 4096
BLOCK, HALF, QUARTER = 512, 256, 128
PIECE, FEW, TALL = 32, 96, 256
COLORS, CORES, LAYERS, ROWS, DEVICES = 3, 2, 2, 64, 16
WIDTH, FOURTH, TILE = 2 * BLOCK, D // 4, (8, 128)
VMEM = 67_000_000
WEIGHTS = (4, 2, 1)
BOTH = range(CORES)
SPREAD, ZEROS = (CORES,) * 4, (0,) * 5
UNITS = 48
OWN, IN = 8, 6
GATHERS, SLOTS = 38, 10
WIDE, DOWN = ("wide",), ("down",)
HURRY = 34
LAST = 5
LAGS = (LAST, 4, 3, 1, 0)


def span(i, size):
    return pl.ds(pl.multiple_of(i * size, size), size)


def loop(first, last, do):
    def step(i, carry):
        do(i)
        return carry

    lax.fori_loop(first, last, step, 0)


def ids(n):
    return tuple(pl.program_id(i) for i in range(n))


def along(reduce, a):
    return reduce(a, -1, keepdims=True)


def bits_of(chip):
    return tuple(chip // w % 2 for w in WEIGHTS)


def place():
    me = lax.axis_index("dp")
    chip = me // CORES
    bits = bits_of(chip)
    near = tuple(me + CORES * w * (1 - 2 * b) for b, w in zip(bits, WEIGHTS))
    return me % CORES, chip, bits, me + 1 - 2 * (me % CORES), near


def dot(a, b, dims):
    return lax.dot_general(a, b, dims, preferred_element_type=F32)


def normed(h):
    wide = h.astype(F32)
    scale = lax.rsqrt(along(jnp.mean, wide * wide) + 1e-6)
    return (wide * scale).astype(BF)


def adamw(w, m, v, g):
    m = 0.9 * m + 0.1 * g
    v = 0.95 * v + 0.05 * g * g
    step = m * lax.rsqrt(v + 1e-8) + 0.1 * w
    return (w - 0.02 * step).astype(BF), m, v


class Scatter:
    def __init__(self, own, r0, ra, rb, rc, sa, sb, sc, out, squares, sems, free, g_hbm):
        self.own, self.r0, self.ra, self.rb, self.rc = own, r0, ra, rb, rc
        self.sa, self.sb, self.sc, self.out, self.squares = sa, sb, sc, out, squares
        self.sems, self.free, self.g_hbm = sems, free, g_hbm
        self.core, self.chip, self.bits, self.partner, self.near = place()

    def copy(self, phase, src, dst, slot, color, device):
        send, recv = self.sems[phase]
        at = (slot,) if color is None else (slot, color)
        return pltpu.make_async_remote_copy(
            src_ref=src, dst_ref=dst, send_sem=send.at[at], recv_sem=recv.at[at], device_id={"dp": device}, device_id_type=MESH
        )

    def copy_0(self, u):
        slot = lax.rem(u, IN)
        return self.copy(0, self.own.at[lax.rem(u, OWN), 1 - self.core], self.r0.at[slot], slot, None, self.partner)

    def copy_a(self, u, k):
        slot = lax.rem(u, IN)
        return self.copy(1, self.sa.at[slot, k], self.ra.at[slot, k], slot, k, self.near[k])

    def copy_b(self, u, k):
        slot = lax.rem(u, IN)
        return self.copy(2, self.sb.at[slot, k], self.rb.at[slot, k], slot, k, self.near[(k + 1) % COLORS])

    def copy_c(self, u, k):
        slot = lax.rem(u, IN)
        return self.copy(3, self.sc.at[slot, k], self.rc.at[slot, k], slot, k, self.near[(k + 2) % COLORS])

    def write(self, u):
        slot = lax.rem(u, IN)
        return pltpu.make_async_copy(self.out.at[slot], self.g_hbm.at[u], self.sems[4].at[slot])

    def index(self, k, a, b, c):
        return a * WEIGHTS[k] + b * WEIGHTS[(k + 1) % COLORS] + c * WEIGHTS[(k + 2) % COLORS]

    def two(self, u, k, index):
        own = self.own[lax.rem(u, OWN), self.core, index, k].astype(F32)
        return own + self.r0[lax.rem(u, IN), index, k].astype(F32)

    def phase_0(self, u):
        @pl.when(u >= IN)
        def _():
            pl.semaphore_wait(self.free.at[3], 1)

        self.copy_0(u).start()

    def phase_a(self, u):
        @pl.when(u >= IN)
        def _():
            for axis in range(COLORS):
                pl.semaphore_wait(self.free.at[axis], 1)

        self.copy_0(u).wait_recv()
        slot = lax.rem(u, IN)
        for k in range(COLORS):
            away = 1 - self.bits[k]
            for b in BOTH:
                for c in BOTH:
                    self.sa[slot, k, 2 * b + c] = self.two(u, k, self.index(k, away, b, c)).astype(BF)
            self.copy_a(u, k).start()

    def phase_b(self, u):
        slot = lax.rem(u, IN)
        for k in range(COLORS):
            here, away = self.bits[k], 1 - self.bits[(k + 1) % COLORS]
            self.copy_a(u, k).wait_recv()
            for c in BOTH:
                total = self.two(u, k, self.index(k, here, away, c)) + self.ra[slot, k, 2 * away + c].astype(F32)
                self.sb[slot, k, c] = total.astype(BF)
            self.copy_b(u, k).start()

    def phase_c(self, u):
        slot = lax.rem(u, IN)
        for k in range(COLORS):
            a, b, away = self.bits[k], self.bits[(k + 1) % COLORS], 1 - self.bits[(k + 2) % COLORS]
            self.copy_b(u, k).wait_recv()
            total = self.two(u, k, self.index(k, a, b, away)) + self.ra[slot, k, 2 * b + away].astype(F32)
            self.sc[slot, k, 0] = (total + self.rb[slot, k, away].astype(F32)).astype(BF)
            self.copy_c(u, k).start()

    def phase_d(self, u):
        slot = lax.rem(u, IN)

        @pl.when(u >= IN)
        def _():
            self.write(u - IN).wait()

        for k in range(COLORS):
            b, c = self.bits[(k + 1) % COLORS], self.bits[(k + 2) % COLORS]
            self.copy_c(u, k).wait_recv()
            total = self.two(u, k, self.chip) + self.ra[slot, k, 2 * b + c].astype(F32)
            total = total + self.rb[slot, k, c].astype(F32) + self.rc[slot, k, 0].astype(F32)
            rounded = total.astype(BF)
            self.out[slot, pl.ds(PIECE * k, PIECE), :] = rounded
            wide = rounded.astype(F32)
            square = wide * wide
            self.squares[:] += square[0:8] + square[8:16] + square[16:24] + square[24:PIECE]
        self.write(u).start()
        self.copy_0(u).wait_send()
        for k in range(COLORS):
            self.copy_a(u, k).wait_send()
            self.copy_b(u, k).wait_send()
            self.copy_c(u, k).wait_send()

        @pl.when(u + IN < UNITS)
        def _():
            pl.semaphore_signal(self.free.at[3], inc=1, device_id={"dp": self.partner}, device_id_type=MESH)
            for axis in range(COLORS):
                pl.semaphore_signal(self.free.at[axis], inc=1, device_id={"dp": self.near[axis]}, device_id_type=MESH)

    def tick(self, q, low, high):
        for lag, phase in zip(LAGS, (self.phase_d, self.phase_c, self.phase_b, self.phase_a, self.phase_0)):
            u = q - lag

            @pl.when((u >= low) & (u < high))
            def _(phase=phase, u=u):
                phase(u)


class Gather:
    def __init__(self, wide, down, sems):
        self.wide, self.down, self.sems = wide, down, sems
        self.core, _, self.bits, self.partner, self.near = place()

    def by_kind(self, n, do, kinds=WIDE + DOWN, when=True):
        layer, at = n // 19, lax.rem(n, 19)

        def wide(chips, core, color=None):
            rows = pl.ds(0, FEW) if color is None else pl.ds(PIECE * color, PIECE)
            return self.wide.at[2 * layer + lax.rem(at, 2), *chips, core, rows, span(at // 2, BLOCK)]

        def down(chips, core, color=None):
            rows = pl.ds(0, HALF) if color is None else pl.ds(88 * color, (88, 88, 80)[color])
            return self.down.at[layer, *chips, core, rows, span((at - 16), BLOCK)]

        inside = (n >= 0) & (n < GATHERS) & when
        for kind, piece in (("wide", wide), ("down", down)):
            if kind in kinds:
                mine = True if len(kinds) == 1 else at < 16 if kind == "wide" else at >= 16
                pl.when(inside & mine)(functools.partial(do, piece))

    def copy(self, phase, n, k, at, device):
        send, recv = self.sems[phase]
        slot = lax.rem(n, SLOTS)
        return pltpu.make_async_remote_copy(
            src_ref=at, dst_ref=at, send_sem=send.at[slot, k], recv_sem=recv.at[slot, k], device_id={"dp": device}, device_id_type=MESH
        )

    def copies(self, phase, n, piece, coming=False):
        found = []
        for k in range(COLORS):
            order = (k, (k + 1) % COLORS, (k + 2) % COLORS)
            chips = list(self.bits)
            if coming:
                chips[order[phase]] = 1 - chips[order[phase]]
            for axis in order[:phase]:
                chips[axis] = slice(None)
            found.append(self.copy(phase, n, k, piece(chips, self.core, k), self.near[order[phase]]))
        return found

    def across(self, n, piece, core):
        return self.copy(3, n, 0, piece([slice(None)] * 3, core), self.partner)

    def first(self, n, kinds=WIDE + DOWN, when=True):
        def do(piece):
            for c in self.copies(0, n, piece):
                c.start()

        self.by_kind(n, do, kinds, when)

    def hop(self, phase, n, kinds, when):
        def do(piece):
            for c in self.copies(phase - 1, n, piece, coming=True):
                c.wait_recv()
            for c in self.copies(phase, n, piece):
                c.start()

        self.by_kind(n, do, kinds, when)

    def middle(self, n, kinds=WIDE + DOWN, when=True):
        self.hop(1, n, kinds, when)

    def last(self, n, kinds=WIDE + DOWN, when=True):
        self.hop(2, n, kinds, when)

    def send(self, n, kinds=WIDE + DOWN):
        self.first(n + 4, kinds, n + 4 <= HURRY)
        self.middle(n + 2, kinds, n + 2 <= HURRY)
        self.last(n, kinds, n <= HURRY)

    def share(self, n, kinds=WIDE + DOWN):
        def do(piece):
            for c in self.copies(2, n, piece, coming=True):
                c.wait_recv()
            self.across(n, piece, self.core).start()
            for phase in range(COLORS):
                for c in self.copies(phase, n, piece):
                    c.wait_send()

        self.by_kind(n, do, kinds)

    def arrive(self, n, kinds=WIDE + DOWN):
        def do(piece):
            self.across(n, piece, 1 - self.core).wait_recv()
            self.across(n, piece, self.core).wait_send()

        self.by_kind(n, do, kinds)


class Plan:
    def __init__(self):
        self.first, self.low, self.made, self.log = LAST, 0, 0, []

    def stage(self, at, steps, units_before):
        stage = (self.first, self.low, self.made)
        for j in range(steps):
            if j in at:
                self.log.append((self.first, self.low, self.made + units_before(j)))
                self.first += 1
            for u in range(self.made + units_before(j), self.made + units_before(j + 1)):
                assert u - OWN < self.low or u - OWN <= self.log[-1][0] - LAST, u
        self.made += units_before(steps)
        return stage

    def restart(self, idle):
        assert self.first - LAST >= self.made, (self.first, self.made)
        self.first, self.low = self.made - idle, self.made

    def check(self):
        seen = {}
        for q, low, high in self.log:
            for name, lag in zip("dcba0", LAGS):
                u = q - lag
                if low <= u < high:
                    seen.setdefault(u, []).append(name)
        assert all(seen.get(u) == list("0abcd") for u in range(UNITS)), seen


def step_kernel(
    x, dy, w_gate, w_up, w_down,
    wide, down, g_all, u_all, act_all, a_all, h1, d_all, g_hbm, total_ref,
    x1, own, r0, ra, rb, rc, sa, sb, sc, out, squares, sums, sum_all,
    s0s, s0r, sas, sar, sbs, sbr, scs, scr, out_sem, free, sum_send, sum_recv, load_sem, act_sem, own_sem,
    *gather_sems,
):
    me = lax.axis_index("dp")
    barrier = pltpu.get_barrier_semaphore()
    for other in range(1, DEVICES):
        pl.semaphore_signal(barrier, inc=1, device_id={"dp": (me + other) % DEVICES}, device_id_type=MESH)
    pl.semaphore_wait(barrier, 15)

    gather = Gather(wide, down, tuple(zip(gather_sems[::2], gather_sems[1::2])))
    scatter = Scatter(own, r0, ra, rb, rc, sa, sb, sc, out, squares, ((s0s, s0r), (sas, sar), (sbs, sbr), (scs, scr), out_sem), free, g_hbm)
    squares[:] = jnp.zeros_like(squares)
    load = pltpu.make_async_copy(dy, x1, load_sem.at[0])

    def own_blocks(gate, up, low, then):
        taken = [pltpu.make_async_copy(a, b, own_sem.at[i]) for i, (a, b) in enumerate(((w_gate, gate), (w_up, up), (w_down, low)))]
        for c in taken:
            c.start()
        at, put = (*gather.bits, gather.core), []
        for i, held in enumerate((gate, up, low)):
            taken[i].wait()
            for layer in BOTH:
                to = down.at[layer, *at] if i == 2 else wide.at[2 * layer + i, *at]
                put.append(pltpu.make_async_copy(held.at[layer], to, own_sem.at[3 + 2 * i + layer]))
                put[-1].start()
        for c in put[0::2]:
            c.wait()
        then()
        for c in put[1::2]:
            c.wait()

    def norm(a):
        def some(i):
            at = span(i, ROWS)
            a[at, :] = normed(x1[at, :])

        loop(0, M // ROWS, some)

    def up_and_gate(a, layer, aside):
        unit, second = 19 * layer, layer > 0
        gather.share(unit + 1, WIDE)
        gather.arrive(unit, WIDE)
        gather.arrive(unit + 1, WIDE)

        def step(wg_ref, wu_ref, g_ref, u_ref, act_ref):
            c, m = ids(2)
            following = unit + 2 * c + 2

            @pl.when(((m == 0) | (m == 3)) & (c < 6))
            def _():
                gather.send(following + 3 + m // 3)

            @pl.when((m == 3) & (c > 5) & ~second)
            def _():
                gather.send(11 + c)

            @pl.when(second & (c == 5) & (m == 0))
            def _():
                for late in range(HURRY + 1, GATHERS):
                    gather.first(late, DOWN)

            @pl.when(second & (c == 7) & (m < 3))
            def _():
                gather.middle(HURRY + 1 + m, DOWN)

            @pl.when((m == 1) & (c < 7))
            def _():
                gather.share(following, WIDE)
                gather.share(following + 1, WIDE)

            @pl.when((m == 2) & (c == 7) & ~second)
            def _():
                gather.share(c + 9, DOWN)

            @pl.when((m == 3) & (c == 2))
            def _():
                aside()

            for s in BOTH:
                rows = pl.ds(HALF * s, HALF)
                mine = a[pl.ds(pl.multiple_of(m * BLOCK, BLOCK) + HALF * s, HALF), :]
                gate = jnp.dot(mine, wg_ref[:].reshape(D, BLOCK), preferred_element_type=F32)
                g_ref[rows, :] = gate
                up = jnp.dot(mine, wu_ref[:].reshape(D, BLOCK), preferred_element_type=F32)
                u_ref[rows, :] = up
                act_ref[rows, :] = (gate * lax.logistic(gate) * up).astype(BF)

            @pl.when((m == 2) & (c < 7))
            def _():
                gather.arrive(following, WIDE)
                gather.arrive(following + 1, WIDE)

        weight = pl.BlockSpec((*SPREAD, FEW, BLOCK), lambda c, m: (*ZEROS, c))
        tile = pl.BlockSpec((BLOCK, BLOCK), lambda c, m: (m, c))
        pltpu.emit_pipeline(step, grid=(8, 4), in_specs=[weight, weight], out_specs=[tile] * 3)(
            wide.at[2 * layer], wide.at[2 * layer + 1], g_all.at[layer], u_all.at[layer], act_all.at[layer]
        )

    def lower():
        def step(act_ref, w_ref):
            p, m = ids(2)

            @pl.when(m == 0)
            def _():
                gather.send(19 + p, WIDE)

            @pl.when((p == 2) & (m > 1))
            def _():
                gather.send(20 + m, WIDE)

            @pl.when((m == 1) & (p < 2))
            def _():
                gather.share(17 + p, DOWN)

            columns = span(p, BLOCK)
            for s in BOTH:
                w = w_ref[:].reshape(F, BLOCK)
                by = jnp.dot(act_ref[HALF * s : HALF * s + HALF, :], w, preferred_element_type=F32).astype(BF)
                rows = pl.ds(pl.multiple_of(m * BLOCK, BLOCK) + HALF * s, HALF)
                x1[rows, columns] = (x1[rows, columns].astype(F32) + by.astype(F32)).astype(BF)

            @pl.when((m == 2) & (p < 2))
            def _():
                gather.arrive(17 + p, DOWN)

        gather.arrive(16, DOWN)
        weight = pl.BlockSpec((*SPREAD, TALL, BLOCK), lambda p, m: (*ZEROS, p))
        pltpu.emit_pipeline(step, grid=(3, 4), in_specs=[pl.BlockSpec((BLOCK, F), lambda p, m: (m, 0)), weight], out_specs=[])(
            act_all.at[0], down.at[0]
        )

    def forward(x2):
        take = pltpu.make_async_copy(x, x1, load_sem.at[0])
        take.start()
        keep_h1 = pltpu.make_async_copy(x1, h1, load_sem.at[2])

        def begin(i):
            gather.send(i, WIDE)

        def then():
            gather.first(0, WIDE)
            gather.first(1, WIDE)

        def own(gate, up, low):
            own_blocks(gate, up, low, then)

        with jax.named_scope("begin"):
            pl.run_scoped(own, pltpu.VMEM((2, FEW, F), BF), pltpu.VMEM((2, FEW, F), BF), pltpu.VMEM((2, HALF, D), BF))
            for unit in BOTH:
                gather.first(unit + 2, WIDE)
                gather.middle(unit, WIDE)
            take.wait()
            norm(x2)
            loop(0, 5, begin)
            gather.share(0, WIDE)

        def layer(number):
            keep_a = pltpu.make_async_copy(x2, a_all.at[number], load_sem.at[1])
            keep_a.start()

            def aside():
                keep_a.wait()

                @pl.when(number == 1)
                def _():
                    keep_h1.wait()
                    load.start()

            with jax.named_scope("up_and_gate"):
                up_and_gate(x2, number, aside)

            @pl.when(number == 0)
            def _():
                with jax.named_scope("lower"):
                    lower()
                with jax.named_scope("norm"):
                    gather.share(19, WIDE)
                    norm(x2)
                keep_h1.start()


        loop(0, 2, layer)

    def down_gradient(layer, made, stage):
        def body(held):
            def block(f):
                return pltpu.make_async_copy(
                    act_all.at[layer, :, span(f, BLOCK)], held.at[f], act_sem.at[f]
                )

            for f in range(8):
                block(f).start()
            second = layer > 0
            pl.when(second)(load.wait)

            def step(t):
                third, quarter = t // 4, lax.rem(t, 4)

                @pl.when(second & (t < 3))
                def _():
                    gather.last(HURRY + 1 + t, DOWN)

                @pl.when(second & ((t == 5) | (t == 8) | (t == 11)))
                def _():
                    gather.share(HURRY + t // 3, DOWN)

                @pl.when(t < 4)
                def _():
                    block(2 * quarter).wait()
                    block(2 * quarter + 1).wait()

                @pl.when(lax.rem(t, 2) == 0)
                def _():
                    scatter.tick(stage[0] + t // 2, stage[1], stage[2] + third * 8 // 3)

                for b in BOTH:
                    f = 2 * quarter + b
                    tile = dot(held[f], x1[:, span(third, BLOCK)], TN).astype(BF)
                    for rows in range(8):
                        piece = third * 8 + rows
                        for core in BOTH:
                            row = HALF * core + PIECE * rows
                            own[lax.rem(made + piece // 3, OWN), core, f, lax.rem(piece, 3), :, :] = tile[row : row + PIECE, :]

            loop(0, 12, step)

        pl.run_scoped(body, pltpu.VMEM((8, M, BLOCK), BF))

    def hidden(x2, layer, made, stage):
        def step(w_ref, g_ref, u_ref, dg_ref, du_ref):
            f, phase = ids(2)
            seen = stage[2] + 2 * f

            @pl.when((phase == 0) | (phase == 2) | ((phase == 3) & ((f == 0) | (f == 2))))
            def _():
                at = 5 * (f // 2) + 3 * lax.rem(f, 2) + phase - phase // 2
                at = jnp.where(f < 4, at, 2 + 2 * f + phase // 2)
                scatter.tick(stage[0] + at, stage[1], seen + phase // 3)

            @pl.when(phase < 2)
            def _():
                for s in range(4):
                    rows = pl.ds(HALF * s, HALF)
                    here = span(4 * phase + s, HALF)
                    by = dot(x1[here, :], w_ref[:].reshape(BLOCK, D), NT).astype(BF).astype(F32)
                    gate, up = g_ref[rows, :], u_ref[rows, :]
                    sigmoid = lax.logistic(gate)
                    silu = gate * sigmoid
                    du_ref[here, :] = (by * silu).astype(BF)
                    dg_ref[here, :] = (by * up * (sigmoid + silu * (1.0 - sigmoid))).astype(BF)

            def unit(by_ref, which):
                slot = lax.rem(made + 2 * f + which, OWN)
                for b in range(4):
                    tile = dot(x2[:, FOURTH * b : FOURTH * b + FOURTH], by_ref[:], TN).astype(BF)
                    for s in range(4):
                        for k in range(COLORS):
                            row = FEW * s + PIECE * k
                            own[slot, s % 2, 2 * b + s // 2, k, :, :] = tile[row : row + PIECE, :]

            pl.when(phase == 2)(lambda: unit(dg_ref, 0))
            pl.when(phase == 3)(lambda: unit(du_ref, 1))

        tile = pl.BlockSpec((WIDTH, BLOCK), lambda f, phase: (jnp.minimum(phase, 1), f), pipeline_mode=pl.Buffered(3))
        all_rows = pl.BlockSpec((M, BLOCK), lambda f, phase: (0, f))
        weight = pl.BlockSpec((1, 1, 1, 2, HALF, D), lambda f, phase: (*bits_of(f), *ZEROS[:3]))
        pltpu.emit_pipeline(step, grid=(8, 4), in_specs=[weight, tile, tile], out_specs=[all_rows, all_rows])(
            down.at[layer], g_all.at[layer], u_all.at[layer], d_all.at[0, layer], d_all.at[1, layer]
        )

    def states(stage):
        def body(da, held):
            def step(d_ref, w_ref):
                m, which, n = ids(3)
                first, end = (which == 0) & (n == 0), (which == 1) & (n == 1)
                take = pltpu.make_async_copy(h1.at[span(m, BLOCK)], held, load_sem.at[2])

                @pl.when(first)
                def _():
                    take.start()

                scatter.tick(stage[0] + 4 * m + 2 * which + n, stage[1], stage[2])
                by = dot(d_ref[:].reshape(BLOCK, F), w_ref[:].reshape(768, F), NT).astype(BF)

                @pl.when(which == 0)
                def _():
                    da[n] = by

                @pl.when(which > 0)
                def _():
                    da[n] = (da[n].astype(F32) + by.astype(F32)).astype(BF)

                @pl.when(end)
                def _():
                    take.wait()

                    def some(i):
                        at = span(i, ROWS)
                        wide = held[at, :].astype(F32)
                        scale = lax.rsqrt(along(jnp.mean, wide * wide) + 1e-6)
                        by = jnp.concatenate([da[n, at, :] for n in BOTH], axis=-1).astype(F32)
                        inner = along(jnp.sum, by * wide)
                        back = (by * scale - wide * (inner * scale * scale * scale * (1.0 / D))).astype(BF)
                        at_all = span(8 * m + i, ROWS)
                        x1[at_all, :] = (x1[at_all, :].astype(F32) + back.astype(F32)).astype(BF)

                    loop(0, 8, some)

            tile = pl.BlockSpec((1, BLOCK, F), lambda m, which, n: (which, m, 0))
            rows = pl.BlockSpec((1, 1, *SPREAD[:3], FEW, F), lambda m, which, n: (2 + which, n, *ZEROS))
            pltpu.emit_pipeline(step, grid=(4, 2, 2), in_specs=[tile, rows], out_specs=[])(d_all.at[:, 1], wide)

        pl.run_scoped(body, pltpu.VMEM((2, BLOCK, 768), BF), pltpu.VMEM((BLOCK, D), BF))

    plan, stages = Plan(), {}
    for layer in (1, 0):
        plan.restart(2)
        stages["down", layer] = plan.stage(range(0, 12, 2), 12, lambda t: t // 4 * 8 // 3)
        at = [4 * f + phase for f in range(8) for phase in ((0, 2, 3) if f in (0, 2) else (0, 2))]
        stages["hidden", layer] = plan.stage(at, PIECE, lambda j: j // 4 * 2 + j % 4 // 3)
        if layer:
            stages["states"] = plan.stage(range(16), 16, lambda j: 0)
    left = UNITS + LAST - plan.first
    first_left, low_left, _ = plan.stage(range(left), left, lambda j: 0)
    plan.check()

    def backward(i):
        layer, made = 1 - i, 24 * i

        def chosen(name):
            return tuple(jnp.where(i == 0, a, b) for a, b in zip(stages[name, 1], stages[name, 0]))

        def gradients(x2):
            take = pltpu.make_async_copy(a_all.at[layer], x2, load_sem.at[1])
            take.start()
            with jax.named_scope("down_gradient"):
                down_gradient(layer, made, chosen("down"))

            @pl.when(layer == 1)
            def _():
                def one(n):
                    gather.arrive(n, DOWN)

                loop(35, 38, one)

            take.wait()
            with jax.named_scope("hidden"):
                hidden(x2, layer, made + 8, chosen("hidden"))

        pl.run_scoped(gradients, pltpu.VMEM((M, D), BF))
        @pl.when(layer == 1)
        def _():
            with jax.named_scope("states"):
                states(stages["states"])


    pl.run_scoped(forward, pltpu.VMEM((M, D), BF))
    loop(0, 2, backward)

    def rest(t):
        scatter.tick(first_left + t, low_left, UNITS)

    with jax.named_scope("rest"):
        loop(0, left, rest)

    def last(u):
        scatter.write(u).wait()

    loop(UNITS - IN, UNITS, last)

    mine = jnp.sum(squares[:], axis=(0, 1), keepdims=True)
    sums[:] = jnp.broadcast_to(mine, sums.shape)

    def tell(to, of):
        return pltpu.make_async_remote_copy(
            src_ref=sums, dst_ref=sum_all.at[of], send_sem=sum_send.at[to], recv_sem=sum_recv.at[of], device_id={"dp": to}, device_id_type=MESH
        )

    for other in range(1, DEVICES):
        tell((me + other) % DEVICES, me).start()
    for other in range(1, DEVICES):
        tell((me + other) % DEVICES, (me + other) % DEVICES).wait_recv()
    for other in range(1, DEVICES):
        tell((me + other) % DEVICES, me).wait_send()
    sum_all[me] = sums[:]
    total = sum_all[0]
    for i in range(1, DEVICES):
        total = total + sum_all[i]
    total_ref[:] = total


def one_step(*args):
    any_spec = pl.BlockSpec(memory_space=pl.ANY)
    shape = jax.ShapeDtypeStruct
    piece = (COLORS, PIECE, BLOCK)
    dma = pltpu.SemaphoreType.DMA
    sums = [pltpu.VMEM((IN, COLORS, n, PIECE, BLOCK), BF) for n in (4, 2, 1)]
    outs = [
        shape((4, *SPREAD, FEW, F), BF), shape((LAYERS, *SPREAD, TALL, D), BF), shape((LAYERS, M, F), F32), shape((LAYERS, M, F), F32),
        shape((LAYERS, M, F), BF), shape((LAYERS, M, D), BF), shape((M, D), BF), shape((CORES, LAYERS, M, F), BF),
    ]
    outs = pl.pallas_call(
        step_kernel,
        out_shape=[*outs, shape((UNITS, FEW, BLOCK), BF), shape(TILE, F32)],
        in_specs=[any_spec] * 5,
        out_specs=[any_spec] * (len(outs) + 1) + [pl.BlockSpec(memory_space=pltpu.VMEM)],
        scratch_shapes=[
            pltpu.VMEM((M, D), BF),
            pltpu.VMEM((OWN, CORES, 8, *piece), BF),
            pltpu.VMEM((IN, 8, *piece), BF), *sums, *sums,
            pltpu.VMEM((IN, FEW, BLOCK), BF), pltpu.VMEM((8, BLOCK), F32), pltpu.VMEM(TILE, F32), pltpu.VMEM((DEVICES, *TILE), F32),
            dma((IN,)), dma((IN,)), *[dma((IN, COLORS))] * 6, dma((IN,)), pltpu.SemaphoreType.REGULAR((4,)),
            dma((DEVICES,)), dma((DEVICES,)), *[dma((9,))] * 3, *[dma((SLOTS, COLORS))] * 8,
        ],
        compiler_params=pltpu.CompilerParams(collective_id=0, has_side_effects=True, vmem_limit_bytes=VMEM),
        cost_estimate=pl.CostEstimate(flops=15 * 2 * M * D * F, bytes_accessed=900_000_000, transcendentals=0),
        name="training_step",
    )(*args)
    return outs[-2], outs[-1]


def adamw_kernel(total, *refs):
    count = LAYERS * COLORS * D * F
    factor = jnp.minimum(1.0, 0.5 * lax.rsqrt(total[:1, :1] / count + 1e-30))
    for i in range(COLORS):
        w, m, v, g, new_w, new_m, new_v = refs[i::COLORS]
        blocks = [(b, pl.ds(0, FEW), pl.ds(BLOCK * b, BLOCK)) for b in BOTH]
        if i == 2:
            blocks = [((c, r), pl.ds(PIECE * r, PIECE), pl.ds(BLOCK * c, BLOCK)) for c in range(COLORS) for r in BOTH]
        for at, rows, columns in blocks:
            by = (g[0, at, 0] if i < 2 else g[0, at[0], at[1]]).astype(F32) * factor
            new_w[0, rows, columns], new_m[0, rows, columns], new_v[0, rows, columns] = adamw(
                w[0, rows, columns].astype(F32), m[0, rows, columns], v[0, rows, columns], by
            )


def optimizer(total, weights, m, v, units):
    wide = pl.BlockSpec((1, FEW, WIDTH), lambda layer, i: (layer, 0, i))
    down = pl.BlockSpec((1, ROWS, D), lambda layer, i: (layer, i, 0))
    blocks = [wide, wide, down]

    def order(which):
        return lambda layer, i: (1 - layer, 2 + i, which, 0, 0)

    gradients = [pl.BlockSpec((1, 2, 1, FEW, BLOCK), order(0)), pl.BlockSpec((1, 2, 1, FEW, BLOCK), order(1))]
    gradients.append(pl.BlockSpec((1, 3, 2, PIECE, BLOCK), lambda layer, i: (1 - layer, 0, i, 0, 0)))
    by_columns, by_rows = units.reshape(2, 12, 2, FEW, BLOCK), units.reshape(2, 9, 8, PIECE, BLOCK)
    return pl.pallas_call(
        adamw_kernel,
        grid=(2, 4),
        out_shape=[jax.ShapeDtypeStruct(w.shape, BF) for w in weights] + [jax.ShapeDtypeStruct(a.shape, F32) for a in (*m, *v)],
        in_specs=[pl.BlockSpec(TILE, lambda layer, i: (0, 0)), *blocks * 3, *gradients],
        out_specs=blocks * 3,
        compiler_params=pltpu.CompilerParams(vmem_limit_bytes=VMEM),
        name="optimizer",
    )(total, *weights, *m, *v, by_columns, by_columns, by_rows)


def solution(mesh):
    def step(x, dy, *arrays):
        weights, m, v = (arrays[i : i + 3] for i in (0, 3, 6))
        units, total = one_step(x[0], dy[0], *weights)
        return tuple(optimizer(total, weights, m, v, units))

    states, cut = P(("rep", "dp"), None, None), P(None, "dp", None)
    return jax.shard_map(
        step,
        mesh=mesh,
        in_specs=(states, states) + (cut,) * 9,
        out_specs=(P("rep", "dp", None),) * 9,
        check_vma=False,
    )
```

time: 1210 us -> 661 us (0.55)
  Pallas kernels: 0 us -> 660 us
  matrix products: 573 us -> 0 us
  waiting for transfers between devices: 513 us -> 0 us
  other arithmetic: 36 us -> 0 us
  local copies, waits for them, and re-layouts: 33 us -> 0 us
  blocking collectives: 31.8 us -> 0 us
  between operations: 17.5 us -> 0.83 us
    pallas_call x0 -> x2, Pallas kernels: none -> 660 us  [the longest x1 642 us: one_step(): pl.pallas_call(step_kernel, out_shape=[*outs, shape((UNITS, FEW, BLOCK),...]
    dot_general x15 -> x0, matrix products: 573 us -> none  [the longest x5 198 us: layer(): gate = jnp.dot(a, w['w_gate'], preferred_element_type=jnp.float32)]
    reduce_scatter x6 -> x0, waiting for transfers between devices: 342 us -> none  [step(): lax.psum_scatter(by_w[name], 'dp', scatter_dimension=0, tiled=True)]
    all_gather x6 -> x0, waiting for transfers between devices: 170 us -> none  [fetched(): lax.all_gather(w[number], 'dp', axis=0, tiled=True)]
    psum x1 -> x0, blocking collectives: 31.8 us -> none  [step(): squares = lax.psum(sum((jnp.sum(g * g) for g in gradients)), 'dp')]
    unnamed x38 -> x0, local copies, waits for them, and re-layouts: 25 us -> none
    convert_element_type x2 -> x0, other arithmetic: 14.7 us -> none  [adamw(): return ((w - 0.02 * step).astype(jnp.bfloat16), m, v)]
    reduce_sum x4 -> x0, other arithmetic: 12.6 us -> none  [the longest x3 8.5 us: step(): squares = lax.psum(sum((jnp.sum(g * g) for g in gradients)), 'dp')]
  transfers between devices with their start and end apart: 12 -> 0, of which waited for: 10 -> 0; matrix products, arithmetic and copies ran while one was open for 37% -> 0% of each run, Pallas kernels for 0% -> 0%
where the time goes in v2:
time: 661 us
  Pallas kernels  660 us (100%)
    pallas_call x1, Pallas kernels, one_step(): pl.pallas_call(step_kernel, out_shape=[*outs, shape((UNITS, FEW, BLOCK),...  642 us
    pallas_call x1, Pallas kernels, optimizer(): pl.pallas_call(adamw_kernel, grid=(2, 4), out_shape=[jax.ShapeDtypeStruct...  18.3 us

profile of v2, /device:TPU:0, one launch (start us, length us, event | category | flops | bytes accessed | tf_op | source)
XLA Modules:
  0.0 661.1 jit_solution(3424500654195047148)
XLA Ops:
  0.6 641.9 %training_step.1 = (bf16[4,2,2,2,2,96,4096]{6,5,4,3,2,1,0:T(8,128)(2,1)}, bf16[2,2,2,2,2,256,1536]{6,5,4,3,2,1,0:T(8,128)(2,1)}, f32[2,2048,4096]{2,1,0:T(8,128)...) custom-call(bf16[2048,1536]{1,0:T(8,128)(2,1)} %bitcast.7, ...), custom_call_target="tpu_custom_call" | custom-call | flops 386547056640 | bytes 900000000 | tf_op jit(solution)/shard_map/training_step/pallas_call | solution.py:727
  642.6 18.3 %optimizer.1 = (bf16[2,96,4096]{2,1,0:T(8,128)(2,1)}, bf16[2,96,4096]{2,1,0:T(8,128)(2,1)}, bf16[2,256,1536]{2,1,0:T(8,128)(2,1)}, f32[2,96,4096]{2,1,0:T(8,128)...) custom-call(f32[8,128]{1,0:T(8,128)} %get-tuple-element.11.total, ...), custom_call_target="tpu_custom_call" | custom-call | tf_op jit(solution)/shard_map/optimizer/pallas_call | solution.py:773

commit v3 on v2

--- a/solution.py
+++ b/solution.py
@@ -222,11 +222,11 @@
                 mine = True if len(kinds) == 1 else at < 16 if kind == "wide" else at >= 16
                 pl.when(inside & mine)(functools.partial(do, piece))
 
-    def copy(self, phase, n, k, at, device):
+    def copy(self, phase, n, k, at, device, source=None):
         send, recv = self.sems[phase]
         slot = lax.rem(n, SLOTS)
         return pltpu.make_async_remote_copy(
-            src_ref=at, dst_ref=at, send_sem=send.at[slot, k], recv_sem=recv.at[slot, k], device_id={"dp": device}, device_id_type=MESH
+            src_ref=at if source is None else source, dst_ref=at, send_sem=send.at[slot, k], recv_sem=recv.at[slot, k], device_id={"dp": device}, device_id_type=MESH
         )
 
     def copies(self, phase, n, piece, coming=False):
@@ -250,6 +250,11 @@
                 c.start()
 
         self.by_kind(n, do, kinds, when)
+
+    def begin(self, n, source):
+        for k in range(COLORS):
+            at = self.wide.at[n, *self.bits, self.core, pl.ds(PIECE * k, PIECE), pl.ds(0, BLOCK)]
+            self.copy(0, n, k, at, self.near[k], source.at[0, pl.ds(PIECE * k, PIECE), pl.ds(0, BLOCK)]).start()
 
     def hop(self, phase, n, kinds, when):
         def do(piece):
@@ -337,7 +342,7 @@
     squares[:] = jnp.zeros_like(squares)
     load = pltpu.make_async_copy(dy, x1, load_sem.at[0])
 
-    def own_blocks(gate, up, low, then):
+    def own_blocks(gate, up, low):
         taken = [pltpu.make_async_copy(a, b, own_sem.at[i]) for i, (a, b) in enumerate(((w_gate, gate), (w_up, up), (w_down, low)))]
         for c in taken:
             c.start()
@@ -348,10 +353,7 @@
                 to = down.at[layer, *at] if i == 2 else wide.at[2 * layer + i, *at]
                 put.append(pltpu.make_async_copy(held.at[layer], to, own_sem.at[3 + 2 * i + layer]))
                 put[-1].start()
-        for c in put[0::2]:
-            c.wait()
-        then()
-        for c in put[1::2]:
+        for c in put:
             c.wait()
 
     def norm(a):
@@ -405,10 +407,12 @@
                 rows = pl.ds(HALF * s, HALF)
                 mine = a[pl.ds(pl.multiple_of(m * BLOCK, BLOCK) + HALF * s, HALF), :]
                 gate = jnp.dot(mine, wg_ref[:].reshape(D, BLOCK), preferred_element_type=F32)
-                g_ref[rows, :] = gate
+                sigmoid = lax.logistic(gate)
+                silu = gate * sigmoid
+                u_ref[rows, :] = silu
                 up = jnp.dot(mine, wu_ref[:].reshape(D, BLOCK), preferred_element_type=F32)
-                u_ref[rows, :] = up
-                act_ref[rows, :] = (gate * lax.logistic(gate) * up).astype(BF)
+                g_ref[rows, :] = up * (sigmoid + silu * (1.0 - sigmoid))
+                act_ref[rows, :] = (silu * up).astype(BF)
 
             @pl.when((m == 2) & (c < 7))
             def _():
@@ -462,15 +466,10 @@
         def begin(i):
             gather.send(i, WIDE)
 
-        def then():
-            gather.first(0, WIDE)
-            gather.first(1, WIDE)
-
-        def own(gate, up, low):
-            own_blocks(gate, up, low, then)
-
         with jax.named_scope("begin"):
-            pl.run_scoped(own, pltpu.VMEM((2, FEW, F), BF), pltpu.VMEM((2, FEW, F), BF), pltpu.VMEM((2, HALF, D), BF))
+            gather.begin(0, w_gate)
+            gather.begin(1, w_up)
+            pl.run_scoped(own_blocks, pltpu.VMEM((2, FEW, F), BF), pltpu.VMEM((2, FEW, F), BF), pltpu.VMEM((2, HALF, D), BF))
             for unit in BOTH:
                 gather.first(unit + 2, WIDE)
                 gather.middle(unit, WIDE)
@@ -564,15 +563,12 @@
 
             @pl.when(phase < 2)
             def _():
-                for s in range(4):
-                    rows = pl.ds(HALF * s, HALF)
-                    here = span(4 * phase + s, HALF)
+                for s in BOTH:
+                    rows = pl.ds(BLOCK * s, BLOCK)
+                    here = span(CORES * phase + s, BLOCK)
                     by = dot(x1[here, :], w_ref[:].reshape(BLOCK, D), NT).astype(BF).astype(F32)
-                    gate, up = g_ref[rows, :], u_ref[rows, :]
-                    sigmoid = lax.logistic(gate)
-                    silu = gate * sigmoid
-                    du_ref[here, :] = (by * silu).astype(BF)
-                    dg_ref[here, :] = (by * up * (sigmoid + silu * (1.0 - sigmoid))).astype(BF)
+                    du_ref[here, :] = (by * u_ref[rows, :]).astype(BF)
+                    dg_ref[here, :] = (by * g_ref[rows, :]).astype(BF)
 
             def unit(by_ref, which):
                 slot = lax.rem(made + 2 * f + which, OWN)

time: 661 us -> 653 us (0.988)
  Pallas kernels: 660 us -> 652 us
    pallas_call x1, Pallas kernels: 642 us -> 634 us  [one_step(): pl.pallas_call(step_kernel, out_shape=[*outs, shape((UNITS, FEW, BLOCK),...]
where the time goes in v3:
time: 653 us
  Pallas kernels  652 us (100%)
    pallas_call x1, Pallas kernels, one_step(): pl.pallas_call(step_kernel, out_shape=[*outs, shape((UNITS, FEW, BLOCK),...  634 us
    pallas_call x1, Pallas kernels, optimizer(): pl.pallas_call(adamw_kernel, grid=(2, 4), out_shape=[jax.ShapeDtypeStruct...  18.3 us

profile of v3, /device:TPU:0, one launch (start us, length us, event | category | flops | bytes accessed | tf_op | source)
XLA Modules:
  0.0 653.3 jit_solution(4315907227232026609)
XLA Ops:
  0.6 634.2 %training_step.1 = (bf16[4,2,2,2,2,96,4096]{6,5,4,3,2,1,0:T(8,128)(2,1)}, bf16[2,2,2,2,2,256,1536]{6,5,4,3,2,1,0:T(8,128)(2,1)}, f32[2,2048,4096]{2,1,0:T(8,128)...) custom-call(bf16[2048,1536]{1,0:T(8,128)(2,1)} %bitcast.7, ...), custom_call_target="tpu_custom_call" | custom-call | flops 386547056640 | bytes 900000000 | tf_op jit(solution)/shard_map/training_step/pallas_call | solution.py:723
  634.8 18.3 %optimizer.1 = (bf16[2,96,4096]{2,1,0:T(8,128)(2,1)}, bf16[2,96,4096]{2,1,0:T(8,128)(2,1)}, bf16[2,256,1536]{2,1,0:T(8,128)(2,1)}, f32[2,96,4096]{2,1,0:T(8,128)...) custom-call(f32[8,128]{1,0:T(8,128)} %get-tuple-element.11.total, ...), custom_call_target="tpu_custom_call" | custom-call | tf_op jit(solution)/shard_map/optimizer/pallas_call | solution.py:769
